TPU v7x, 256 devices: a whole 4x4x8 slice. The times are simulated.
256 devices in a mesh: orb: 64 (over x, z, core), rep: 4 (over y).
Axes of the slice: x: 4, y: 4, z: 8, core: 2. Of those that a mesh axis runs over, the one named last changes fastest.
Arguments:
- orbitals: float32 [128, 64, 4096], P('orb'), may hold values from -6 to 6
- pair_list: int32 [1024, 3], P(('orb', 'rep')), may hold values from 0 to 127, as said below
- box_offsets: int32 [128, 3], replicated, may hold values from 0 to 1023, as said below
Outputs:
- exchange_forces: float32 [128, 64, 4096], P('orb')
- slab_field: float32 [1024, 9216], P('orb')
Inputs may be any that keep to these rules, and one draw needn't show every extreme that they name: `pair_list`: the rows of one device are the 4 slots of block d, blocks in order of orb then rep. Their first orbital belongs to orbital group g = d // 4 (numbers g * 2 to g * 2 + 1); their second belongs to group g - 1, g or g + 1. The live flag is 1 on the first 1 to 4 rows of each block and 0 after; in every draw some block is all live. `box_offsets`: orbital k's z offset lies from (k // 2) * 16 to that plus 16 - 1; its x and y offsets lie from 0 to 31.
All inputs are finite; a program needn't handle non-finite values.
Results may differ from a plain program's by a relative error of at most 0.0003.
Values sent between devices are 32-bit elements; how exact they have to be, the bound alone decides.
No kernel may reach another device: no remote copies, remote signals or barrier semaphores. Data moves between devices by JAX's collectives and lax.ppermute only.
A program may use at most 128 MiB of HBM per device.

v0:
```python
import functools

import jax
import jax.numpy as jnp
import numpy as np
from jax import lax
from jax.experimental import pallas as pl
from jax.experimental.pallas import tpu as pltpu
from jax.sharding import PartitionSpec as P


BOX = 64
SLAB = 16
WIDE = 96
ITERS = 5
SCREEN = 6.1
LANES = 128
COLS = BOX * BOX // LANES
FRONT = 16
GROUP = 16
ROOM = 32
QUARTER = COLS // 4
SLABS = BOX // SLAB + 1
SPAN = WIDE * BOX // 4 + 32 * WIDE
PAIRS_VMEM = 32 * 1024 * 1024
SMALL_VMEM = 12 * 1024 * 1024
SMEM = pl.BlockSpec(memory_space=pltpu.SMEM)
VMEM = pl.BlockSpec(memory_space=pltpu.VMEM)
HBM = pl.BlockSpec(memory_space=pltpu.HBM)


def place():
    return lax.axis_index("orb"), lax.axis_index("rep")


def neighbours(group):
    return group ^ 1, group + 2 * (group & 1) - 1


def lane_of(rows):
    return lax.broadcasted_iota(jnp.int32, (rows, LANES), 1)


def fold(block):
    return jnp.sum(block.reshape(BOX // 8, 8, LANES), axis=0)


def total(partial):
    return jnp.sum(jnp.sum(partial, axis=1, keepdims=True), axis=0, keepdims=True)


def shift_reader(buffer, dz, dx, dy):
    lanes = lane_of(BOX)
    flat = dx * BOX + dy
    blocks = flat >> 7
    turn = flat & (LANES - 1)
    ypos = lanes & (BOX - 1)
    inside = (ypos >= dy) & (ypos < BOX + dy)
    early = lanes < LANES - turn

    def read(c):
        near = buffer[c - blocks + FRONT, pl.ds(ROOM - dz, BOX), :]
        before = buffer[c - blocks + FRONT - 1, pl.ds(ROOM - dz, BOX), :]
        turned = pltpu.roll(jnp.where(early, near, before), turn, 1)
        return jnp.where(inside, turned, 0.0)

    return read


def beside(field, c, center, after, within):
    above = field[c + 1, pl.ds(9, BOX), :]
    below = field[c + 1, pl.ds(7, BOX), :]
    ahead = field[c, pl.ds(8, BOX), :]
    across = pltpu.roll(jnp.where(lane_of(BOX) < BOX, after, ahead), BOX, 1)
    high = center.astype(jnp.bfloat16)
    low = (center - high.astype(jnp.float32)).astype(jnp.bfloat16)
    inner = jnp.dot(jnp.concatenate([high, low], axis=1), within[...], preferred_element_type=jnp.float32)
    return (inner + across) + (above + below)


def columns(c):
    return pl.ds(pl.multiple_of(c * LANES, LANES), LANES)


def load_box(own, other, which, write):
    for boxes, first in ((own, 0), (other, 2)):

        @pl.when((which >= first) & (which < first + 2))
        def _():
            def block(c, carry):
                write(c, boxes[which - first, :, columns(c)])
                return carry

            lax.fori_loop(0, COLS, block, 0, unroll=8)


def solve_pair(own, other, first, second, delta, within, buffer, still, shifted, basis, image):
    def to_buffer(c, block):
        buffer[c + FRONT, pl.ds(ROOM, BOX), :] = block

    def to_still(c, block):
        still[c] = block

    load_box(own, other, first, to_buffer)
    load_box(own, other, second, to_still)
    read = shift_reader(buffer, *delta)
    diagonal, coupling = [], []
    norm_before = None
    for k in range(ITERS):
        field = basis.at[k]

        def value_of(c):
            if k == 0:
                moved = read(c)
                shifted[c] = moved
                return still[c] * moved
            fresh = image[c] - diagonal[k - 1] * basis[k - 1, c + 1, pl.ds(8, BOX), :]
            if k > 1:
                fresh = fresh - coupling[k - 1] * basis[k - 2, c + 1, pl.ds(8, BOX), :]
            return fresh

        def group(start, carry, final):
            norm, cross = carry
            center = field[start + 1, pl.ds(8, BOX), :]
            values = [center]
            for u in range(1, GROUP + 1):
                if final and u == GROUP:
                    values.append(jnp.zeros_like(center))
                    continue
                fresh = value_of(start + u)
                field[start + u + 1, pl.ds(8, BOX), :] = fresh
                norm = norm + fold(fresh * fresh)
                values.append(fresh)
            for u in range(GROUP):
                result = beside(field, start + u, values[u], values[u + 1], within)
                if k < ITERS - 1:
                    image[start + u] = result
                cross = cross + fold(values[u] * result)
            return norm, cross

        opening = value_of(0)
        field[1, pl.ds(8, BOX), :] = opening
        carry = (fold(opening * opening), jnp.zeros((8, LANES), jnp.float32))
        carry = lax.fori_loop(0, COLS // GROUP - 1, lambda m, held: group(m * GROUP, held, False), carry)
        norm, cross = group(COLS - GROUP, carry, True)
        norm = total(norm)
        diagonal.append(total(cross) / norm)
        coupling.append(norm / norm_before if k > 0 else None)
        norm_before = norm
    pivots = [SCREEN - diagonal[0]]
    rights = [jnp.ones_like(pivots[0])]
    for k in range(1, ITERS):
        pivots.append(SCREEN - diagonal[k] - coupling[k] / pivots[k - 1])
        rights.append(rights[k - 1] / pivots[k - 1])
    weights = [None] * ITERS
    weights[ITERS - 1] = rights[ITERS - 1] / pivots[ITERS - 1]
    for k in range(ITERS - 2, -1, -1):
        weights[k] = (rights[k] + coupling[k + 1] * weights[k + 1]) / pivots[k]
    return weights


def run_pair(own, other, first, second, delta, to_second, to_first, within, forces, *scratch):
    buffer, still, shifted, basis, image = scratch
    weights = solve_pair(own, other, first, second, delta, within, *scratch)

    def finish(c, carry):
        potential = weights[0] * basis[0, c + 1, pl.ds(8, BOX), :]
        for k in range(1, ITERS):
            potential = potential + weights[k] * basis[k, c + 1, pl.ds(8, BOX), :]
        image[c] = potential
        buffer[c + FRONT, pl.ds(ROOM, BOX), :] = potential * still[c]
        return carry

    lax.fori_loop(0, COLS, finish, 0, unroll=4)

    @pl.when(to_second)
    def _():
        def deposit(c, carry):
            forces[second, c] = forces[second, c] + image[c] * shifted[c]
            return carry

        lax.fori_loop(0, COLS, deposit, 0, unroll=4)

    @pl.when(to_first)
    def _():
        read = shift_reader(buffer, -delta[0], -delta[1], -delta[2])

        def deposit(c, carry):
            forces[first, c] = forces[first, c] + read(c)
            return carry

        lax.fori_loop(0, COLS, deposit, 0, unroll=8)


def pairs_kernel(begun, *refs):
    if begun:
        lists, offsets, own, other, within, tally, forces_in, *parts, forces = refs[:12]
    else:
        lists, offsets, own, other, within, forces, tally_out = refs[:7]
    scratch = refs[-5:]
    buffer, basis = scratch[0], scratch[3]
    group, mine = place()
    near, far = neighbours(group)
    neighbour, which = (far, 2) if begun else (near, 1)

    def clear(c, carry):
        buffer[c] = jnp.zeros((BOX + 2 * ROOM, LANES), jnp.float32)
        return carry

    lax.fori_loop(0, COLS + 2 * FRONT, clear, 0, unroll=4)
    nothing = jnp.zeros((BOX + 16, LANES), jnp.float32)
    for k in range(ITERS):
        basis[k, 0] = nothing
        basis[k, COLS + 1] = nothing

        def clear_ends(c, carry):
            basis[k, c + 1, pl.ds(0, 8), :] = jnp.zeros((8, LANES), jnp.float32)
            basis[k, c + 1, pl.ds(BOX + 8, 8), :] = jnp.zeros((8, LANES), jnp.float32)
            return carry

        lax.fori_loop(0, COLS, clear_ends, 0, unroll=4)

    def open_forces(c, carry):
        for k in range(2):
            forces[k, c] = forces_in[k, c] if begun else jnp.zeros((BOX, LANES), jnp.float32)
        return carry

    lax.fori_loop(0, COLS, open_forces, 0, unroll=2)

    def slot(n, count):
        foreign = n // 16
        row = n % 16
        base = ((row // 4) ^ mine) * 36 + foreign * which * 12 + (row % 4) * 3
        first = lists[base]
        second = lists[base + 1]
        live = lists[base + 2] > 0
        second_group = second // 2
        inner = second_group == group
        outer = second_group == neighbour
        if begun:
            wanted = jnp.where(foreign > 0, inner, outer)
        else:
            wanted = jnp.where(foreign > 0, inner, inner | outer)
        taken = live & wanted
        turn = taken & (lax.rem(count, 4) == mine)

        @pl.when(turn)
        def _():
            delta = [offsets[first * 3 + axis] - offsets[second * 3 + axis] for axis in range(3)]
            first_at = jnp.where(foreign > 0, 2 + first - 2 * neighbour, first - 2 * group)
            second_at = jnp.where(inner, second - 2 * group, 2 + second - 2 * neighbour)
            run_pair(own, other, first_at, second_at, delta, inner, foreign == 0, within, forces, *scratch)

        return count + taken.astype(jnp.int32)

    if not begun:
        tally_out[0] = lax.fori_loop(0, 32, slot, jnp.int32(0))
        return
    lax.fori_loop(0, 32, slot, tally[0])
    for k, side in enumerate((1, 3)):
        for n, who in enumerate((mine ^ side, mine)):
            for half, quarter in enumerate((who, who ^ (4 - side))):
                for c in range(QUARTER):
                    parts[2 * k + n][half * QUARTER + c] = forces[k, quarter * QUARTER + c]


def within_block():
    lane = np.arange(LANES)
    gap = np.abs(lane[:, None] - lane[None, :])
    same_row = lane[:, None] // BOX == lane[None, :] // BOX
    once = ((gap == 1) & same_row) | (gap == BOX)
    return jnp.asarray(np.concatenate([once, once]), jnp.bfloat16)


def stage_kernel(boxes, out):
    pltpu.sync_copy(boxes, out)


def stage(boxes):
    return pl.pallas_call(
        stage_kernel,
        out_shape=jax.ShapeDtypeStruct(boxes.shape, boxes.dtype),
        in_specs=[HBM],
        out_specs=VMEM,
        compiler_params=pltpu.CompilerParams(vmem_limit_bytes=SMALL_VMEM),
        cost_estimate=pl.CostEstimate(flops=1_000_000, bytes_accessed=4 << 20, transcendentals=0),
        name="stage",
    )(boxes)


def run_pairs(lists, offsets, own, other, before=None):
    begun = before is not None
    operands = [lists, offsets, own, other, within_block()]
    in_specs = [SMEM, SMEM, VMEM, VMEM, VMEM]
    whole = (2, COLS, BOX, LANES)
    scratch = [
        pltpu.VMEM((COLS + 2 * FRONT, BOX + 2 * ROOM, LANES), jnp.float32),
        pltpu.VMEM((COLS, BOX, LANES), jnp.float32),
        pltpu.VMEM((COLS, BOX, LANES), jnp.float32),
        pltpu.VMEM((ITERS, COLS + 2, BOX + 16, LANES), jnp.float32),
        pltpu.VMEM((COLS, BOX, LANES), jnp.float32),
    ]
    if begun:
        operands += [before[1], before[0]]
        in_specs += [SMEM, VMEM]
        out_shape = [jax.ShapeDtypeStruct((2 * QUARTER, BOX, LANES), jnp.float32)] * 4
        out_specs = [VMEM] * 4
        scratch = [pltpu.VMEM(whole, jnp.float32)] + scratch
    else:
        out_shape = [jax.ShapeDtypeStruct(whole, jnp.float32), jax.ShapeDtypeStruct((1,), jnp.int32)]
        out_specs = [VMEM, SMEM]
    return pl.pallas_call(
        functools.partial(pairs_kernel, begun),
        out_shape=out_shape,
        in_specs=in_specs,
        out_specs=out_specs,
        scratch_shapes=scratch,
        compiler_params=pltpu.CompilerParams(vmem_limit_bytes=PAIRS_VMEM),
        cost_estimate=pl.CostEstimate(flops=100_000_000, bytes_accessed=8 << 20, transcendentals=0),
        name="pairs_far" if begun else "pairs_near",
    )(*operands)


def settle_kernel(offsets, *refs):
    parts, sums, pieces, tall = refs[:6], refs[6:8], refs[8:13], refs[13]
    group, _ = place()
    for k in range(2):
        kept, once, twice = parts[3 * k : 3 * k + 3]
        tall[:, pl.ds(0, SLAB), :] = jnp.zeros((QUARTER, SLAB, LANES), jnp.float32)
        tall[:, pl.ds(SLAB + BOX, SLAB), :] = jnp.zeros((QUARTER, SLAB, LANES), jnp.float32)
        for c in range(QUARTER):
            value = (kept[c] + once[c]) + twice[c]
            sums[k][c] = value
            tall[c, pl.ds(SLAB, BOX), :] = value
        depth = offsets[(2 * group + k) * 3] - group * SLAB
        for t in range(SLABS):
            for c in range(QUARTER):
                pieces[t][k, c] = tall[c, pl.ds(SLAB * (t + 1) - depth, SLAB), :]


def settle(offsets, parts):
    quarter = jax.ShapeDtypeStruct((QUARTER, BOX, LANES), jnp.float32)
    piece = jax.ShapeDtypeStruct((2, QUARTER, SLAB, LANES), jnp.float32)
    return pl.pallas_call(
        settle_kernel,
        out_shape=[quarter] * 2 + [piece] * SLABS,
        in_specs=[SMEM] + [VMEM] * 6,
        out_specs=[VMEM] * (2 + SLABS),
        scratch_shapes=[pltpu.VMEM((QUARTER, BOX + 2 * SLAB, LANES), jnp.float32)],
        cost_estimate=pl.CostEstimate(flops=4_000_000, bytes_accessed=4 << 20, transcendentals=0),
        compiler_params=pltpu.CompilerParams(vmem_limit_bytes=SMALL_VMEM),
        name="settle",
    )(offsets, *parts)


def deposit_kernel(offsets, *refs):
    pieces, outs, span = refs[:SLABS], refs[SLABS : SLABS + 2], refs[-1]
    group, _ = place()
    lanes = lax.broadcasted_iota(jnp.int32, (SLAB, LANES), 1)
    span[...] = jnp.zeros_like(span)
    for t in range(SLABS):
        owner = (group + lax.axis_size("orb") - t) % lax.axis_size("orb")

        def lay(k, carry):
            at = (2 * owner + k) * 3
            base = offsets[at + 1] * WIDE + offsets[at + 2]
            for c in range(QUARTER):
                value = pieces[t][k, c]
                for row in range(2):
                    start = base + (2 * c + row) * WIDE - row * BOX
                    tile, turn = start >> 7, start & (LANES - 1)
                    kept = (lanes < BOX) if row == 0 else (lanes >= BOX)
                    turned = pltpu.roll(jnp.where(kept, value, 0.0), turn, 1)
                    here = pl.ds(pl.multiple_of(tile * LANES, LANES), LANES)
                    there = pl.ds(pl.multiple_of(tile * LANES + LANES, LANES), LANES)
                    span[:, here] = span[:, here] + jnp.where(lanes >= turn, turned, 0.0)
                    span[:, there] = span[:, there] + jnp.where(lanes < turn, turned, 0.0)
            return carry

        lax.fori_loop(0, 2, lay, 0)
    for half in range(2):
        outs[half][...] = span[pl.ds(8 * half, 8), pl.ds(0, SPAN)]


def deposit(offsets, pieces):
    half = jax.ShapeDtypeStruct((SLAB // 2, SPAN), jnp.float32)
    return pl.pallas_call(
        deposit_kernel,
        out_shape=[half] * 2,
        in_specs=[SMEM] + [VMEM] * SLABS,
        out_specs=[VMEM] * 2,
        scratch_shapes=[pltpu.VMEM((SLAB, SPAN + 4 * LANES), jnp.float32)],
        cost_estimate=pl.CostEstimate(flops=8_000_000, bytes_accessed=2 << 20, transcendentals=0),
        compiler_params=pltpu.CompilerParams(vmem_limit_bytes=SMALL_VMEM),
        name="deposit",
    )(offsets, *pieces)


def quarters_of(mine):
    return mine, mine ^ 1, mine ^ 3, mine ^ 2


def merge_kernel(*refs):
    spans, out = refs[:8], refs[8]
    _, mine = place()
    out[...] = jnp.zeros_like(out)
    for n, quarter in enumerate(quarters_of(mine)):
        where = pl.ds(pl.multiple_of(quarter * (WIDE * BOX // 4), LANES), SPAN)
        for half in range(2):
            rows = pl.ds(8 * half, 8)
            out[rows, where] = out[rows, where] + spans[2 * n + half][...]


def merge(spans):
    return pl.pallas_call(
        merge_kernel,
        out_shape=jax.ShapeDtypeStruct((SLAB, WIDE * WIDE), jnp.float32),
        in_specs=[VMEM] * 8,
        out_specs=VMEM,
        cost_estimate=pl.CostEstimate(flops=1_000_000, bytes_accessed=2 << 20, transcendentals=0),
        compiler_params=pltpu.CompilerParams(vmem_limit_bytes=SMALL_VMEM),
        name="merge",
    )(*spans)


def assemble_kernel(*refs):
    parts, out = refs[:8], refs[8]
    _, mine = place()
    for n, quarter in enumerate(quarters_of(mine)):
        for k in range(2):
            for c in range(QUARTER):
                where = pl.ds(pl.multiple_of((quarter * QUARTER + c) * LANES, LANES), LANES)
                out[k, :, where] = parts[2 * n + k][c]


def assemble(parts):
    return pl.pallas_call(
        assemble_kernel,
        out_shape=jax.ShapeDtypeStruct((2, BOX, BOX * BOX), jnp.float32),
        in_specs=[VMEM] * 8,
        out_specs=VMEM,
        cost_estimate=pl.CostEstimate(flops=1_000_000, bytes_accessed=4 << 20, transcendentals=0),
        compiler_params=pltpu.CompilerParams(vmem_limit_bytes=SMALL_VMEM),
        name="assemble",
    )(*parts)


def across(block, side):
    return lax.ppermute(block, "rep", [(i, i ^ side) for i in range(lax.axis_size("rep"))])


def gather_pair(first, second):
    first_one, first_three = across(first, 1), across(first, 3)
    second_one, second_three = across(second, 1), across(second, 3)
    first_two = across(first_three, 1)
    second_two = across(second_one, 3)
    return [first, second, first_one, second_one, first_three, second_three, first_two, second_two]


def shards(orbitals, pair_list, box_offsets):
    groups = lax.axis_size("orb")
    to_near = [(g, g ^ 1) for g in range(groups)]
    to_far = [(g, neighbours(g)[1]) for g in range(groups) if 0 <= neighbours(g)[1] < groups]
    slots = pair_list.reshape(-1)
    near_slots = lax.ppermute(slots, "orb", to_near)
    far_slots = lax.ppermute(slots, "orb", to_far)
    near = lax.ppermute(orbitals, "orb", to_near)
    far = lax.ppermute(orbitals, "orb", to_far)
    known = jnp.concatenate([slots, near_slots, far_slots])
    lists = jnp.concatenate([known] + [across(known, side) for side in (1, 2, 3)])
    offsets = box_offsets.reshape(-1)
    own = stage(orbitals)
    before = run_pairs(lists, offsets, own, near)
    sent_zero, kept_zero, sent_one, kept_one = run_pairs(lists, offsets, own, far, before)
    got_zero, got_one = across(sent_zero, 1), across(sent_one, 3)
    last_zero = across(kept_zero[QUARTER:] + got_zero[QUARTER:], 3)
    last_one = across(kept_one[QUARTER:] + got_one[QUARTER:], 1)
    settled = settle(offsets, (kept_zero, got_zero, last_zero, kept_one, got_one, last_one))
    pieces = [settled[2]]
    for later in range(1, SLABS):
        route = [(i, (i + later) % groups) for i in range(groups)]
        pieces.append(lax.ppermute(settled[2 + later], "orb", route))
    gathered = gather_pair(settled[0], settled[1])
    forces = assemble(gathered)
    spans = deposit(offsets, pieces)
    gathered = gather_pair(*spans)
    slab = merge(gathered)
    return (forces, slab)


def solution(mesh):
    in_specs = (P("orb", None, None), P(("orb", "rep"), None), P())
    out_specs = (P("orb", None, None), P("orb", None))
    return jax.shard_map(shards, mesh=mesh, in_specs=in_specs, out_specs=out_specs, check_vma=False)
```

profile of v0, /device:TPU:4, one launch (start us, length us, event | category | flops | bytes accessed | tf_op | source)
XLA Modules:
  0.0 146.9 jit_solution(8233201711598386397)
XLA Ops:
  0.7 7.8 %collective-permute-start.5 = (f32[2,64,4096]{2,1,0:T(8,128)}, f32[2,64,4096]{2,1,0:T(8,128)}, u32[]{:S(2)}, u32[]{:S(2)}) collective-permute-start(f32[2,64,4096]{2,1,0:T(8,128)} %boxes.1), channel_id=1, source_target_pairs={{4,8},{8,4},{12,16},{16,12},{20,24},{24,20},{28,32},{32,28},{36,40... | collective-permute-start | bytes 6291464 | tf_op jit(solution)/shard_map/ppermute | solution.py:468
  9.3 1.9 %collective-permute-start.1 = (s32[12]{0:T(128)S(1)}, s32[12]{0:T(128)S(1)}, u32[]{:S(2)}, u32[]{:S(2)}) collective-permute-start(s32[12]{0:T(128)S(1)} %reshape.11), channel_id=1, source_target_pairs={{4,8},{8,4},{12,16},{16,12},{20,24},{24,20},{28,32},{32,28},{36,40... | collective-permute-start | bytes 152 | tf_op jit(solution)/shard_map/ppermute | solution.py:466
  14.1 18.5 %collective-permute-done.1 = s32[12]{0:T(128)S(1)} collective-permute-done((s32[12]{0:T(128)S(1)}, s32[12]{0:T(128)S(1)}, u32[]{:S(2)}, u32[]{:S(2)}) %collective-permute-start.1) | collective-permute-done | bytes 80 | tf_op jit(solution)/shard_map/ppermute | solution.py:466
  32.7 3.0 %collective-permute-start.4 = (s32[36]{0:T(128)S(1)}, s32[36]{0:T(128)S(1)}, u32[]{:S(2)}, u32[]{:S(2)}) collective-permute-start(s32[36]{0:T(128)S(1)} %pad_add_fusion), channel_id=1, source_target_pairs={{0,3},{1,2},{2,1},{3,0},{4,7},{5,6},{6,5},{7,4},{8,11},{9,10},{10,... | collective-permute-start | bytes 440 | tf_op jit(solution)/shard_map/ppermute | solution.py:449
  37.5 3.3 %collective-permute-done.3 = s32[36]{0:T(128)S(1)} collective-permute-done((s32[36]{0:T(128)S(1)}, s32[36]{0:T(128)S(1)}, u32[]{:S(2)}, u32[]{:S(2)}) %collective-permute-start.3) | collective-permute-done | bytes 176 | tf_op jit(solution)/shard_map/ppermute | solution.py:449
  40.9 14.5 %pairs_near.1 = (f32[2,32,64,128]{3,2,1,0:T(8,128)S(1)}, s32[1]{0:T(128)}) custom-call(s32[144]{0:T(256)S(1)} %concatenate.8.refs_0_, s32[384]{0:T(512)S(1)} %reshape.10.refs_1_.offsets, f32[2,64,4096]{2,1,0:T(8,128)S(1)} %stage.1.refs_2_, f32[2,64,4096]{2,1,0:T(8,128)} %collective-permute-done.6.refs_3_, bf16[256,128]{1,0:T(8,128)(2,1)S(1)} %copy-done.1), custom_call_target="tpu_custom_call" | custom-call | flops 100000000 | bytes 8388608 | tf_op jit(solution)/shard_map/pairs_near/pallas_call | solution.py:312
  55.4 9.4 %pairs_far.1 = (f32[16,64,128]{2,1,0:T(8,128)S(1)}, f32[16,64,128]{2,1,0:T(8,128)S(1)}, f32[16,64,128]{2,1,0:T(8,128)S(1)}, f32[16,64,128]{2,1,0:T(8,128)S(1)}) custom-call(s32[144]{0:T(256)S(1)} %concatenate.8.refs_0_, s32[384]{0:T(512)S(1)} %reshape.10.refs_1_.offsets, f32[2,64,4096]{2,1,0:T(8,128)S(1)} %stage.1.refs_2_, ...), custom_call_target="tpu_custom_call" | custom-call | flops 100000000 | bytes 8388608 | tf_op jit(solution)/shard_map/pairs_far/pallas_call | solution.py:312
  65.3 1.8 %collective-permute-start.9 = (f32[16,64,128]{2,1,0:T(8,128)S(1)}, f32[16,64,128]{2,1,0:T(8,128)S(1)}, u32[]{:S(2)}, u32[]{:S(2)}) collective-permute-start(f32[16,64,128]{2,1,0:T(8,128)S(1)} %get-tuple-element.22), channel_id=1, source_target_pairs={{0,3},{1,2},{2,1},{3,0},{4,7},{5,6},{6,5},{7,4},{8,11},{9,10},{10,... | collective-permute-start | bytes 1572872 | tf_op jit(solution)/shard_map/ppermute | solution.py:449
  67.1 8.7 %collective-permute-done.7.refs_1_ = f32[16,64,128]{2,1,0:T(8,128)S(1)} collective-permute-done((f32[16,64,128]{2,1,0:T(8,128)S(1)}, f32[16,64,128]{2,1,0:T(8,128)S(1)}, u32[]{:S(2)}, u32[]{:S(2)}) %collective-permute-start.7) | collective-permute-done | bytes 524320 | tf_op jit(solution)/shard_map/ppermute | solution.py:449
  75.8 3.6 %collective-permute-start.8 = (f32[8,64,128]{2,1,0:T(8,128)S(1)}, f32[8,64,128]{2,1,0:T(8,128)S(1)}, u32[]{:S(2)}, u32[]{:S(2)}) collective-permute-start(f32[8,64,128]{2,1,0:T(8,128)S(1)} %slice_add_fusion.1), channel_id=1, source_target_pairs={{0,3},{1,2},{2,1},{3,0},{4,7},{5,6},{6,5},{7,4},{8,11},{9,10},{10,... | collective-permute-start | bytes 786440 | tf_op jit(solution)/shard_map/ppermute | solution.py:449
  80.1 5.6 %collective-permute-done.8.refs_2_ = f32[8,64,128]{2,1,0:T(8,128)S(1)} collective-permute-done((f32[8,64,128]{2,1,0:T(8,128)S(1)}, f32[8,64,128]{2,1,0:T(8,128)S(1)}, u32[]{:S(2)}, u32[]{:S(2)}) %collective-permute-start.8) | collective-permute-done | bytes 262176 | tf_op jit(solution)/shard_map/ppermute | solution.py:449
  85.7 1.9 %collective-permute-done.10.refs_5_ = f32[8,64,128]{2,1,0:T(8,128)S(1)} collective-permute-done((f32[8,64,128]{2,1,0:T(8,128)S(1)}, f32[8,64,128]{2,1,0:T(8,128)S(1)}, u32[]{:S(2)}, u32[]{:S(2)}) %collective-permute-start.10) | collective-permute-done | bytes 262176 | tf_op jit(solution)/shard_map/ppermute | solution.py:449
  88.3 1.9 %collective-permute-start.13 = (f32[8,64,128]{2,1,0:T(8,128)S(1)}, f32[8,64,128]{2,1,0:T(8,128)S(1)}, u32[]{:S(2)}, u32[]{:S(2)}) collective-permute-start(f32[8,64,128]{2,1,0:T(8,128)S(1)} %get-tuple-element.23.refs_0_), channel_id=1, source_target_pairs={{0,3},{1,2},{2,1},{3,0},{4,7},{5,6},{6,5},{7,4},{8,11},{9,10},{10,... | collective-permute-start | bytes 786440 | tf_op jit(solution)/shard_map/ppermute | solution.py:449
  91.3 4.7 %collective-permute-start.19 = (f32[2,8,16,128]{3,2,1,0:T(8,128)S(1)}, f32[2,8,16,128]{3,2,1,0:T(8,128)S(1)}, u32[]{:S(2)}, u32[]{:S(2)}) collective-permute-start(f32[2,8,16,128]{3,2,1,0:T(8,128)S(1)} %get-tuple-element.28), channel_id=1, source_target_pairs={{0,12},{4,16},{8,20},{12,24},{16,28},{20,32},{24,36},{28,40},{32,4... | collective-permute-start | bytes 393224 | tf_op jit(solution)/shard_map/ppermute | solution.py:482
  96.0 1.7 %collective-permute-start.20 = (f32[2,8,16,128]{3,2,1,0:T(8,128)S(1)}, f32[2,8,16,128]{3,2,1,0:T(8,128)S(1)}, u32[]{:S(2)}, u32[]{:S(2)}) collective-permute-start(f32[2,8,16,128]{3,2,1,0:T(8,128)S(1)} %get-tuple-element.29), channel_id=1, source_target_pairs={{0,16},{4,20},{8,24},{12,28},{16,32},{20,36},{24,40},{28,44},{32,4... | collective-permute-start | bytes 393224 | tf_op jit(solution)/shard_map/ppermute | solution.py:482
  97.7 4.4 %collective-permute-done.18.refs_2_ = f32[2,8,16,128]{3,2,1,0:T(8,128)S(1)} collective-permute-done((f32[2,8,16,128]{3,2,1,0:T(8,128)S(1)}, f32[2,8,16,128]{3,2,1,0:T(8,128)S(1)}, u32[]{:S(2)}, u32[]{:S(2)}) %collective-permute-start.18) | collective-permute-done | bytes 131104 | tf_op jit(solution)/shard_map/ppermute | solution.py:482
  102.2 11.1 %collective-permute-done.19.refs_3_ = f32[2,8,16,128]{3,2,1,0:T(8,128)S(1)} collective-permute-done((f32[2,8,16,128]{3,2,1,0:T(8,128)S(1)}, f32[2,8,16,128]{3,2,1,0:T(8,128)S(1)}, u32[]{:S(2)}, u32[]{:S(2)}) %collective-permute-start.19) | collective-permute-done | bytes 131104 | tf_op jit(solution)/shard_map/ppermute | solution.py:482
  114.6 2.7 %deposit.1 = (f32[8,4608]{1,0:T(8,128)S(1)}, f32[8,4608]{1,0:T(8,128)S(1)}) custom-call(s32[384]{0:T(512)S(1)} %reshape.10.refs_1_.offsets, f32[2,8,16,128]{3,2,1,0:T(8,128)S(1)} %get-tuple-element.25.refs_0_, f32[2,8,16,128]{3,2,1,0:T(8,128)S(1)} %collective-permute-done.17.refs_1_, f32[2,8,16,128]{3,2,1,0:T(8,128)S(1)} %collective-permute-done.18.refs_2_, ...), custom_call_target="tpu_custom_call" | custom-call | flops 8000000 | bytes 2097152 | tf_op jit(solution)/shard_map/deposit/pallas_call | solution.py:387
  117.2 1.9 %collective-permute-start.23 = (f32[8,4608]{1,0:T(8,128)S(1)}, f32[8,4608]{1,0:T(8,128)S(1)}, u32[]{:S(2)}, u32[]{:S(2)}) collective-permute-start(f32[8,4608]{1,0:T(8,128)S(1)} %get-tuple-element.30.refs_0_), channel_id=1, source_target_pairs={{0,3},{1,2},{2,1},{3,0},{4,7},{5,6},{6,5},{7,4},{8,11},{9,10},{10,... | collective-permute-start | bytes 442376 | tf_op jit(solution)/shard_map/ppermute | solution.py:449
  122.0 3.3 %collective-permute-done.23.refs_4_ = f32[8,4608]{1,0:T(8,128)S(1)} collective-permute-done((f32[8,4608]{1,0:T(8,128)S(1)}, f32[8,4608]{1,0:T(8,128)S(1)}, u32[]{:S(2)}, u32[]{:S(2)}) %collective-permute-start.23) | collective-permute-done | bytes 147488 | tf_op jit(solution)/shard_map/ppermute | solution.py:449
  125.3 2.0 %collective-permute-start.11 = (f32[8,64,128]{2,1,0:T(8,128)S(1)}, f32[8,64,128]{2,1,0:T(8,128)S(1)}, u32[]{:S(2)}, u32[]{:S(2)}) collective-permute-start(f32[8,64,128]{2,1,0:T(8,128)S(1)} %get-tuple-element.23.refs_0_), channel_id=1, source_target_pairs={{0,1},{1,0},{2,3},{3,2},{4,5},{5,4},{6,7},{7,6},{8,9},{9,8},{10,11... | collective-permute-start | bytes 786440 | tf_op jit(solution)/shard_map/ppermute | solution.py:449
  127.3 1.9 %collective-permute-start.14 = (f32[8,64,128]{2,1,0:T(8,128)S(1)}, f32[8,64,128]{2,1,0:T(8,128)S(1)}, u32[]{:S(2)}, u32[]{:S(2)}) collective-permute-start(f32[8,64,128]{2,1,0:T(8,128)S(1)} %get-tuple-element.24.refs_1_), channel_id=1, source_target_pairs={{0,3},{1,2},{2,1},{3,0},{4,7},{5,6},{6,5},{7,4},{8,11},{9,10},{10,... | collective-permute-start | bytes 786440 | tf_op jit(solution)/shard_map/ppermute | solution.py:449
  132.2 1.6 %collective-permute-start.26 = (f32[8,4608]{1,0:T(8,128)S(1)}, f32[8,4608]{1,0:T(8,128)S(1)}, u32[]{:S(2)}, u32[]{:S(2)}) collective-permute-start(f32[8,4608]{1,0:T(8,128)S(1)} %collective-permute-done.22.refs_3_), channel_id=1, source_target_pairs={{0,3},{1,2},{2,1},{3,0},{4,7},{5,6},{6,5},{7,4},{8,11},{9,10},{10,... | collective-permute-start | bytes 442376 | tf_op jit(solution)/shard_map/ppermute | solution.py:449
  133.8 10.6 %collective-permute-done.26.refs_7_ = f32[8,4608]{1,0:T(8,128)S(1)} collective-permute-done((f32[8,4608]{1,0:T(8,128)S(1)}, f32[8,4608]{1,0:T(8,128)S(1)}, u32[]{:S(2)}, u32[]{:S(2)}) %collective-permute-start.26) | collective-permute-done | bytes 147488 | tf_op jit(solution)/shard_map/ppermute | solution.py:449
  (48 shorter events, 18.2 us)
Async XLA Ops:
  0.6 40.2 %collective-permute-start.6 = (f32[2,64,4096]{2,1,0:T(8,128)}, f32[2,64,4096]{2,1,0:T(8,128)}, u32[]{:S(2)}, u32[]{:S(2)}) collective-permute-start(f32[2,64,4096]{2,1,0:T(8,128)} %boxes.1), channel_id=1, source_target_pairs={{0,4},{4,0},{8,12},{12,8},{16,20},{20,16},{24,28},{28,24},{32,36},... | collective-permute-start | bytes 6291464 | tf_op jit(solution)/shard_map/ppermute | solution.py:467
  0.7 54.6 %collective-permute-start.5 = (f32[2,64,4096]{2,1,0:T(8,128)}, f32[2,64,4096]{2,1,0:T(8,128)}, u32[]{:S(2)}, u32[]{:S(2)}) collective-permute-start(f32[2,64,4096]{2,1,0:T(8,128)} %boxes.1), channel_id=1, source_target_pairs={{4,8},{8,4},{12,16},{16,12},{20,24},{24,20},{28,32},{32,28},{36,40... | collective-permute-start | bytes 6291464 | tf_op jit(solution)/shard_map/ppermute | solution.py:468
  9.3 23.3 %collective-permute-start.1 = (s32[12]{0:T(128)S(1)}, s32[12]{0:T(128)S(1)}, u32[]{:S(2)}, u32[]{:S(2)}) collective-permute-start(s32[12]{0:T(128)S(1)} %reshape.11), channel_id=1, source_target_pairs={{4,8},{8,4},{12,16},{16,12},{20,24},{24,20},{28,32},{32,28},{36,40... | collective-permute-start | bytes 152 | tf_op jit(solution)/shard_map/ppermute | solution.py:466
  11.2 21.3 %collective-permute-start = (s32[12]{0:T(128)S(1)}, s32[12]{0:T(128)S(1)}, u32[]{:S(2)}, u32[]{:S(2)}) collective-permute-start(s32[12]{0:T(128)S(1)} %reshape.11), channel_id=1, source_target_pairs={{0,4},{4,0},{8,12},{12,8},{16,20},{20,16},{24,28},{28,24},{32,36},... | collective-permute-start | bytes 152 | tf_op jit(solution)/shard_map/ppermute | solution.py:465
  64.8 11.0 %collective-permute-start.7 = (f32[16,64,128]{2,1,0:T(8,128)S(1)}, f32[16,64,128]{2,1,0:T(8,128)S(1)}, u32[]{:S(2)}, u32[]{:S(2)}) collective-permute-start(f32[16,64,128]{2,1,0:T(8,128)S(1)} %get-tuple-element.20), channel_id=1, source_target_pairs={{0,1},{1,0},{2,3},{3,2},{4,5},{5,4},{6,7},{7,6},{8,9},{9,8},{10,11... | collective-permute-start | bytes 1572872 | tf_op jit(solution)/shard_map/ppermute | solution.py:449
  65.3 14.2 %collective-permute-start.9 = (f32[16,64,128]{2,1,0:T(8,128)S(1)}, f32[16,64,128]{2,1,0:T(8,128)S(1)}, u32[]{:S(2)}, u32[]{:S(2)}) collective-permute-start(f32[16,64,128]{2,1,0:T(8,128)S(1)} %get-tuple-element.22), channel_id=1, source_target_pairs={{0,3},{1,2},{2,1},{3,0},{4,7},{5,6},{6,5},{7,4},{8,11},{9,10},{10,... | collective-permute-start | bytes 1572872 | tf_op jit(solution)/shard_map/ppermute | solution.py:449
  75.8 9.8 %collective-permute-start.8 = (f32[8,64,128]{2,1,0:T(8,128)S(1)}, f32[8,64,128]{2,1,0:T(8,128)S(1)}, u32[]{:S(2)}, u32[]{:S(2)}) collective-permute-start(f32[8,64,128]{2,1,0:T(8,128)S(1)} %slice_add_fusion.1), channel_id=1, source_target_pairs={{0,3},{1,2},{2,1},{3,0},{4,7},{5,6},{6,5},{7,4},{8,11},{9,10},{10,... | collective-permute-start | bytes 786440 | tf_op jit(solution)/shard_map/ppermute | solution.py:449
  79.5 8.0 %collective-permute-start.10 = (f32[8,64,128]{2,1,0:T(8,128)S(1)}, f32[8,64,128]{2,1,0:T(8,128)S(1)}, u32[]{:S(2)}, u32[]{:S(2)}) collective-permute-start(f32[8,64,128]{2,1,0:T(8,128)S(1)} %slice_add_fusion), channel_id=1, source_target_pairs={{0,1},{1,0},{2,3},{3,2},{4,5},{5,4},{6,7},{7,6},{8,9},{9,8},{10,11... | collective-permute-start | bytes 786440 | tf_op jit(solution)/shard_map/ppermute | solution.py:449
  88.3 32.3 %collective-permute-start.13 = (f32[8,64,128]{2,1,0:T(8,128)S(1)}, f32[8,64,128]{2,1,0:T(8,128)S(1)}, u32[]{:S(2)}, u32[]{:S(2)}) collective-permute-start(f32[8,64,128]{2,1,0:T(8,128)S(1)} %get-tuple-element.23.refs_0_), channel_id=1, source_target_pairs={{0,3},{1,2},{2,1},{3,0},{4,7},{5,6},{6,5},{7,4},{8,11},{9,10},{10,... | collective-permute-start | bytes 786440 | tf_op jit(solution)/shard_map/ppermute | solution.py:449
  90.1 7.6 %collective-permute-start.17 = (f32[2,8,16,128]{3,2,1,0:T(8,128)S(1)}, f32[2,8,16,128]{3,2,1,0:T(8,128)S(1)}, u32[]{:S(2)}, u32[]{:S(2)}) collective-permute-start(f32[2,8,16,128]{3,2,1,0:T(8,128)S(1)} %get-tuple-element.26), channel_id=1, source_target_pairs={{0,4},{4,8},{8,12},{12,16},{16,20},{20,24},{24,28},{28,32},{32,36}... | collective-permute-start | bytes 393224 | tf_op jit(solution)/shard_map/ppermute | solution.py:482
  90.6 11.6 %collective-permute-start.18 = (f32[2,8,16,128]{3,2,1,0:T(8,128)S(1)}, f32[2,8,16,128]{3,2,1,0:T(8,128)S(1)}, u32[]{:S(2)}, u32[]{:S(2)}) collective-permute-start(f32[2,8,16,128]{3,2,1,0:T(8,128)S(1)} %get-tuple-element.27), channel_id=1, source_target_pairs={{0,8},{4,12},{8,16},{12,20},{16,24},{20,28},{24,32},{28,36},{32,40... | collective-permute-start | bytes 393224 | tf_op jit(solution)/shard_map/ppermute | solution.py:482
  91.3 22.0 %collective-permute-start.19 = (f32[2,8,16,128]{3,2,1,0:T(8,128)S(1)}, f32[2,8,16,128]{3,2,1,0:T(8,128)S(1)}, u32[]{:S(2)}, u32[]{:S(2)}) collective-permute-start(f32[2,8,16,128]{3,2,1,0:T(8,128)S(1)} %get-tuple-element.28), channel_id=1, source_target_pairs={{0,12},{4,16},{8,20},{12,24},{16,28},{20,32},{24,36},{28,40},{32,4... | collective-permute-start | bytes 393224 | tf_op jit(solution)/shard_map/ppermute | solution.py:482
  96.0 18.6 %collective-permute-start.20 = (f32[2,8,16,128]{3,2,1,0:T(8,128)S(1)}, f32[2,8,16,128]{3,2,1,0:T(8,128)S(1)}, u32[]{:S(2)}, u32[]{:S(2)}) collective-permute-start(f32[2,8,16,128]{3,2,1,0:T(8,128)S(1)} %get-tuple-element.29), channel_id=1, source_target_pairs={{0,16},{4,20},{8,24},{12,28},{16,32},{20,36},{24,40},{28,44},{32,4... | collective-permute-start | bytes 393224 | tf_op jit(solution)/shard_map/ppermute | solution.py:482
  97.7 27.6 %collective-permute-start.12 = (f32[8,64,128]{2,1,0:T(8,128)S(1)}, f32[8,64,128]{2,1,0:T(8,128)S(1)}, u32[]{:S(2)}, u32[]{:S(2)}) collective-permute-start(f32[8,64,128]{2,1,0:T(8,128)S(1)} %get-tuple-element.24.refs_1_), channel_id=1, source_target_pairs={{0,1},{1,0},{2,3},{3,2},{4,5},{5,4},{6,7},{7,6},{8,9},{9,8},{10,11... | collective-permute-start | bytes 786440 | tf_op jit(solution)/shard_map/ppermute | solution.py:449
  117.2 8.0 %collective-permute-start.23 = (f32[8,4608]{1,0:T(8,128)S(1)}, f32[8,4608]{1,0:T(8,128)S(1)}, u32[]{:S(2)}, u32[]{:S(2)}) collective-permute-start(f32[8,4608]{1,0:T(8,128)S(1)} %get-tuple-element.30.refs_0_), channel_id=1, source_target_pairs={{0,3},{1,2},{2,1},{3,0},{4,7},{5,6},{6,5},{7,4},{8,11},{9,10},{10,... | collective-permute-start | bytes 442376 | tf_op jit(solution)/shard_map/ppermute | solution.py:449
  119.2 8.1 %collective-permute-start.21 = (f32[8,4608]{1,0:T(8,128)S(1)}, f32[8,4608]{1,0:T(8,128)S(1)}, u32[]{:S(2)}, u32[]{:S(2)}) collective-permute-start(f32[8,4608]{1,0:T(8,128)S(1)} %get-tuple-element.30.refs_0_), channel_id=1, source_target_pairs={{0,1},{1,0},{2,3},{3,2},{4,5},{5,4},{6,7},{7,6},{8,9},{9,8},{10,11... | collective-permute-start | bytes 442376 | tf_op jit(solution)/shard_map/ppermute | solution.py:449
  119.2 10.0 %collective-permute-start.24 = (f32[8,4608]{1,0:T(8,128)S(1)}, f32[8,4608]{1,0:T(8,128)S(1)}, u32[]{:S(2)}, u32[]{:S(2)}) collective-permute-start(f32[8,4608]{1,0:T(8,128)S(1)} %get-tuple-element.31.refs_1_), channel_id=1, source_target_pairs={{0,3},{1,2},{2,1},{3,0},{4,7},{5,6},{6,5},{7,4},{8,11},{9,10},{10,... | collective-permute-start | bytes 442376 | tf_op jit(solution)/shard_map/ppermute | solution.py:449
  120.6 8.6 %collective-permute-start.22 = (f32[8,4608]{1,0:T(8,128)S(1)}, f32[8,4608]{1,0:T(8,128)S(1)}, u32[]{:S(2)}, u32[]{:S(2)}) collective-permute-start(f32[8,4608]{1,0:T(8,128)S(1)} %get-tuple-element.31.refs_1_), channel_id=1, source_target_pairs={{0,1},{1,0},{2,3},{3,2},{4,5},{5,4},{6,7},{7,6},{8,9},{9,8},{10,11... | collective-permute-start | bytes 442376 | tf_op jit(solution)/shard_map/ppermute | solution.py:449
  125.3 7.0 %collective-permute-start.25 = (f32[8,4608]{1,0:T(8,128)S(1)}, f32[8,4608]{1,0:T(8,128)S(1)}, u32[]{:S(2)}, u32[]{:S(2)}) collective-permute-start(f32[8,4608]{1,0:T(8,128)S(1)} %collective-permute-done.23.refs_4_), channel_id=1, source_target_pairs={{0,1},{1,0},{2,3},{3,2},{4,5},{5,4},{6,7},{7,6},{8,9},{9,8},{10,11... | collective-permute-start | bytes 442376 | tf_op jit(solution)/shard_map/ppermute | solution.py:449
  125.3 20.1 %collective-permute-start.11 = (f32[8,64,128]{2,1,0:T(8,128)S(1)}, f32[8,64,128]{2,1,0:T(8,128)S(1)}, u32[]{:S(2)}, u32[]{:S(2)}) collective-permute-start(f32[8,64,128]{2,1,0:T(8,128)S(1)} %get-tuple-element.23.refs_0_), channel_id=1, source_target_pairs={{0,1},{1,0},{2,3},{3,2},{4,5},{5,4},{6,7},{7,6},{8,9},{9,8},{10,11... | collective-permute-start | bytes 786440 | tf_op jit(solution)/shard_map/ppermute | solution.py:449
  127.3 18.1 %collective-permute-start.14 = (f32[8,64,128]{2,1,0:T(8,128)S(1)}, f32[8,64,128]{2,1,0:T(8,128)S(1)}, u32[]{:S(2)}, u32[]{:S(2)}) collective-permute-start(f32[8,64,128]{2,1,0:T(8,128)S(1)} %get-tuple-element.24.refs_1_), channel_id=1, source_target_pairs={{0,3},{1,2},{2,1},{3,0},{4,7},{5,6},{6,5},{7,4},{8,11},{9,10},{10,... | collective-permute-start | bytes 786440 | tf_op jit(solution)/shard_map/ppermute | solution.py:449
  129.2 16.2 %collective-permute-start.15 = (f32[8,64,128]{2,1,0:T(8,128)S(1)}, f32[8,64,128]{2,1,0:T(8,128)S(1)}, u32[]{:S(2)}, u32[]{:S(2)}) collective-permute-start(f32[8,64,128]{2,1,0:T(8,128)S(1)} %collective-permute-done.13.refs_4_), channel_id=1, source_target_pairs={{0,1},{1,0},{2,3},{3,2},{4,5},{5,4},{6,7},{7,6},{8,9},{9,8},{10,11... | collective-permute-start | bytes 786440 | tf_op jit(solution)/shard_map/ppermute | solution.py:449
  129.2 16.2 %collective-permute-start.16 = (f32[8,64,128]{2,1,0:T(8,128)S(1)}, f32[8,64,128]{2,1,0:T(8,128)S(1)}, u32[]{:S(2)}, u32[]{:S(2)}) collective-permute-start(f32[8,64,128]{2,1,0:T(8,128)S(1)} %collective-permute-done.12.refs_3_), channel_id=1, source_target_pairs={{0,3},{1,2},{2,1},{3,0},{4,7},{5,6},{6,5},{7,4},{8,11},{9,10},{10,... | collective-permute-start | bytes 786440 | tf_op jit(solution)/shard_map/ppermute | solution.py:449
  132.2 12.2 %collective-permute-start.26 = (f32[8,4608]{1,0:T(8,128)S(1)}, f32[8,4608]{1,0:T(8,128)S(1)}, u32[]{:S(2)}, u32[]{:S(2)}) collective-permute-start(f32[8,4608]{1,0:T(8,128)S(1)} %collective-permute-done.22.refs_3_), channel_id=1, source_target_pairs={{0,3},{1,2},{2,1},{3,0},{4,7},{5,6},{6,5},{7,4},{8,11},{9,10},{10,... | collective-permute-start | bytes 442376 | tf_op jit(solution)/shard_map/ppermute | solution.py:449
  (5 other events, 42.8 us)
where the time goes:
time: 147 us
  waiting for transfers between devices  70.9 us (48%)
  starting transfers between devices  41.7 us (28%)
  Pallas kernels  29.9 us (20%)
  local copies, waits for them, and re-layouts  3.43 us (2%)
    ppermute x19, waiting for transfers between devices, across(): lax.ppermute(block, 'rep', [(i, i ^ side) for i in range(lax.axis_size('r...  35.6 us
    ppermute x19, starting transfers between devices, across(): lax.ppermute(block, 'rep', [(i, i ^ side) for i in range(lax.axis_size('r...  24.2 us
    pallas_call x2, Pallas kernels, run_pairs(): pl.pallas_call(functools.partial(pairs_kernel, begun), out_shape=out_shap...  23.9 us
    ppermute x1, waiting for transfers between devices, shards(): far_slots = lax.ppermute(slots, 'orb', to_far)  18.5 us
    ppermute x4, waiting for transfers between devices, shards(): pieces.append(lax.ppermute(settled[2 + later], 'orb', route))  16.8 us
    ppermute x1, starting transfers between devices, shards(): far = lax.ppermute(orbitals, 'orb', to_far)  7.83 us
    ppermute x4, starting transfers between devices, shards(): pieces.append(lax.ppermute(settled[2 + later], 'orb', route))  7.56 us
  transfers between devices with their start and end apart: 27, of which 12 were waited for; matrix products, arithmetic and copies ran while one was open for 1% of the time, Pallas kernels for 12%

commit v1 on v0

--- a/solution.py
+++ b/solution.py
@@ -194,14 +194,16 @@
 
 def pairs_kernel(begun, *refs):
     if begun:
-        lists, offsets, own, other, within, tally, forces_in, *parts, forces = refs[:12]
+        lists, offsets, own, other_far, within, tally, forces_in, *parts, forces = refs[:12]
     else:
-        lists, offsets, own, other, within, forces, tally_out = refs[:7]
-    scratch = refs[-5:]
+        lists, offsets, own, other_far, within, forces, tally_out = refs[:7]
+    other, other_sem, *scratch = refs[-7:]
     buffer, basis = scratch[0], scratch[3]
     group, mine = place()
     near, far = neighbours(group)
     neighbour, which = (far, 2) if begun else (near, 1)
+    copy = pltpu.make_async_copy(other_far, other, other_sem)
+    copy.start()
 
     def clear(c, carry):
         buffer[c] = jnp.zeros((BOX + 2 * ROOM, LANES), jnp.float32)
@@ -211,7 +213,6 @@
     nothing = jnp.zeros((BOX + 16, LANES), jnp.float32)
     for k in range(ITERS):
         basis[k, 0] = nothing
-        basis[k, COLS + 1] = nothing
 
         def clear_ends(c, carry):
             basis[k, c + 1, pl.ds(0, 8), :] = jnp.zeros((8, LANES), jnp.float32)
@@ -226,15 +227,16 @@
         return carry
 
     lax.fori_loop(0, COLS, open_forces, 0, unroll=2)
+    copy.wait()
 
     def slot(n, count):
-        foreign = n // 16
-        row = n % 16
-        base = ((row // 4) ^ mine) * 36 + foreign * which * 12 + (row % 4) * 3
+        foreign = n >> 4
+        row = n & 15
+        base = ((row >> 2) ^ mine) * 36 + foreign * (which * 12) + (row & 3) * 3
         first = lists[base]
         second = lists[base + 1]
         live = lists[base + 2] > 0
-        second_group = second // 2
+        second_group = second >> 1
         inner = second_group == group
         outer = second_group == neighbour
         if begun:
@@ -242,7 +244,7 @@
         else:
             wanted = jnp.where(foreign > 0, inner, inner | outer)
         taken = live & wanted
-        turn = taken & (lax.rem(count, 4) == mine)
+        turn = taken & ((count & 3) == mine)
 
         @pl.when(turn)
         def _():
@@ -291,13 +293,15 @@
 def run_pairs(lists, offsets, own, other, before=None):
     begun = before is not None
     operands = [lists, offsets, own, other, within_block()]
-    in_specs = [SMEM, SMEM, VMEM, VMEM, VMEM]
+    in_specs = [SMEM, SMEM, VMEM, HBM, VMEM]
     whole = (2, COLS, BOX, LANES)
     scratch = [
+        pltpu.VMEM((2, BOX, BOX * BOX), jnp.float32),
+        pltpu.SemaphoreType.DMA,
         pltpu.VMEM((COLS + 2 * FRONT, BOX + 2 * ROOM, LANES), jnp.float32),
         pltpu.VMEM((COLS, BOX, LANES), jnp.float32),
         pltpu.VMEM((COLS, BOX, LANES), jnp.float32),
-        pltpu.VMEM((ITERS, COLS + 2, BOX + 16, LANES), jnp.float32),
+        pltpu.VMEM((ITERS, COLS + 1, BOX + 16, LANES), jnp.float32),
         pltpu.VMEM((COLS, BOX, LANES), jnp.float32),
     ]
     if begun:

time: 147 us -> 145 us (0.986)
  no operation moved by 1% of the time
where the time goes in v1:
time: 145 us
  waiting for transfers between devices  69.8 us (48%)
  starting transfers between devices  42.3 us (29%)
  Pallas kernels  28.7 us (20%)
  local copies, waits for them, and re-layouts  3.43 us (2%)
    ppermute x19, waiting for transfers between devices, across(): lax.ppermute(block, 'rep', [(i, i ^ side) for i in range(lax.axis_size('r...  35.1 us
    ppermute x19, starting transfers between devices, across(): lax.ppermute(block, 'rep', [(i, i ^ side) for i in range(lax.axis_size('r...  24.8 us
    pallas_call x2, Pallas kernels, run_pairs(): pl.pallas_call(functools.partial(pairs_kernel, begun), out_shape=out_shap...  22.7 us
    ppermute x1, waiting for transfers between devices, shards(): far_slots = lax.ppermute(slots, 'orb', to_far)  18.5 us
    ppermute x4, waiting for transfers between devices, shards(): pieces.append(lax.ppermute(settled[2 + later], 'orb', route))  16.3 us
    ppermute x1, starting transfers between devices, shards(): far = lax.ppermute(orbitals, 'orb', to_far)  7.83 us
    ppermute x4, starting transfers between devices, shards(): pieces.append(lax.ppermute(settled[2 + later], 'orb', route))  7.59 us
  transfers between devices with their start and end apart: 27, of which 12 were waited for; matrix products, arithmetic and copies ran while one was open for 1% of the time, Pallas kernels for 12%

profile of v1, /device:TPU:4, one launch (start us, length us, event | category | flops | bytes accessed | tf_op | source)
XLA Modules:
  0.0 145.1 jit_solution(3867518963875300855)
XLA Ops:
  0.7 7.8 %collective-permute-start.5 = (f32[2,64,4096]{2,1,0:T(8,128)}, f32[2,64,4096]{2,1,0:T(8,128)}, u32[]{:S(2)}, u32[]{:S(2)}) collective-permute-start(f32[2,64,4096]{2,1,0:T(8,128)} %boxes.1), channel_id=1, source_target_pairs={{4,8},{8,4},{12,16},{16,12},{20,24},{24,20},{28,32},{32,28},{36,40... | collective-permute-start | bytes 6291464 | tf_op jit(solution)/shard_map/ppermute | solution.py:472
  9.3 1.9 %collective-permute-start.1 = (s32[12]{0:T(128)S(1)}, s32[12]{0:T(128)S(1)}, u32[]{:S(2)}, u32[]{:S(2)}) collective-permute-start(s32[12]{0:T(128)S(1)} %reshape.11), channel_id=1, source_target_pairs={{4,8},{8,4},{12,16},{16,12},{20,24},{24,20},{28,32},{32,28},{36,40... | collective-permute-start | bytes 152 | tf_op jit(solution)/shard_map/ppermute | solution.py:470
  14.1 18.5 %collective-permute-done.1 = s32[12]{0:T(128)S(1)} collective-permute-done((s32[12]{0:T(128)S(1)}, s32[12]{0:T(128)S(1)}, u32[]{:S(2)}, u32[]{:S(2)}) %collective-permute-start.1) | collective-permute-done | bytes 80 | tf_op jit(solution)/shard_map/ppermute | solution.py:470
  32.7 3.0 %collective-permute-start.4 = (s32[36]{0:T(128)S(1)}, s32[36]{0:T(128)S(1)}, u32[]{:S(2)}, u32[]{:S(2)}) collective-permute-start(s32[36]{0:T(128)S(1)} %pad_add_fusion), channel_id=1, source_target_pairs={{0,3},{1,2},{2,1},{3,0},{4,7},{5,6},{6,5},{7,4},{8,11},{9,10},{10,... | collective-permute-start | bytes 440 | tf_op jit(solution)/shard_map/ppermute | solution.py:453
  37.5 3.3 %collective-permute-done.3 = s32[36]{0:T(128)S(1)} collective-permute-done((s32[36]{0:T(128)S(1)}, s32[36]{0:T(128)S(1)}, u32[]{:S(2)}, u32[]{:S(2)}) %collective-permute-start.3) | collective-permute-done | bytes 176 | tf_op jit(solution)/shard_map/ppermute | solution.py:453
  40.9 13.9 %pairs_near.1 = (f32[2,32,64,128]{3,2,1,0:T(8,128)S(1)}, s32[1]{0:T(128)}) custom-call(s32[144]{0:T(256)S(1)} %concatenate.8.refs_0_, s32[384]{0:T(512)S(1)} %reshape.10.refs_1_.offsets, f32[2,64,4096]{2,1,0:T(8,128)S(1)} %stage.1.refs_2_, f32[2,64,4096]{2,1,0:T(8,128)} %collective-permute-done.6.refs_3_, bf16[256,128]{1,0:T(8,128)(2,1)S(1)} %copy-done.1), custom_call_target="tpu_custom_call" | custom-call | flops 100000000 | bytes 8388608 | tf_op jit(solution)/shard_map/pairs_near/pallas_call | solution.py:316
  54.8 8.8 %pairs_far.1 = (f32[16,64,128]{2,1,0:T(8,128)S(1)}, f32[16,64,128]{2,1,0:T(8,128)S(1)}, f32[16,64,128]{2,1,0:T(8,128)S(1)}, f32[16,64,128]{2,1,0:T(8,128)S(1)}) custom-call(s32[144]{0:T(256)S(1)} %concatenate.8.refs_0_, s32[384]{0:T(512)S(1)} %reshape.10.refs_1_.offsets, f32[2,64,4096]{2,1,0:T(8,128)S(1)} %stage.1.refs_2_, ...), custom_call_target="tpu_custom_call" | custom-call | flops 100000000 | bytes 8388608 | tf_op jit(solution)/shard_map/pairs_far/pallas_call | solution.py:316
  63.9 1.7 %collective-permute-start.9 = (f32[16,64,128]{2,1,0:T(8,128)S(1)}, f32[16,64,128]{2,1,0:T(8,128)S(1)}, u32[]{:S(2)}, u32[]{:S(2)}) collective-permute-start(f32[16,64,128]{2,1,0:T(8,128)S(1)} %get-tuple-element.22), channel_id=1, source_target_pairs={{0,3},{1,2},{2,1},{3,0},{4,7},{5,6},{6,5},{7,4},{8,11},{9,10},{10,... | collective-permute-start | bytes 1572872 | tf_op jit(solution)/shard_map/ppermute | solution.py:453
  65.7 8.9 %collective-permute-done.7.refs_1_ = f32[16,64,128]{2,1,0:T(8,128)S(1)} collective-permute-done((f32[16,64,128]{2,1,0:T(8,128)S(1)}, f32[16,64,128]{2,1,0:T(8,128)S(1)}, u32[]{:S(2)}, u32[]{:S(2)}) %collective-permute-start.7) | collective-permute-done | bytes 524320 | tf_op jit(solution)/shard_map/ppermute | solution.py:453
  74.6 3.3 %collective-permute-start.8 = (f32[8,64,128]{2,1,0:T(8,128)S(1)}, f32[8,64,128]{2,1,0:T(8,128)S(1)}, u32[]{:S(2)}, u32[]{:S(2)}) collective-permute-start(f32[8,64,128]{2,1,0:T(8,128)S(1)} %slice_add_fusion.1), channel_id=1, source_target_pairs={{0,3},{1,2},{2,1},{3,0},{4,7},{5,6},{6,5},{7,4},{8,11},{9,10},{10,... | collective-permute-start | bytes 786440 | tf_op jit(solution)/shard_map/ppermute | solution.py:453
  78.6 5.9 %collective-permute-done.8.refs_2_ = f32[8,64,128]{2,1,0:T(8,128)S(1)} collective-permute-done((f32[8,64,128]{2,1,0:T(8,128)S(1)}, f32[8,64,128]{2,1,0:T(8,128)S(1)}, u32[]{:S(2)}, u32[]{:S(2)}) %collective-permute-start.8) | collective-permute-done | bytes 262176 | tf_op jit(solution)/shard_map/ppermute | solution.py:453
  86.0 2.9 %collective-permute-start.13 = (f32[8,64,128]{2,1,0:T(8,128)S(1)}, f32[8,64,128]{2,1,0:T(8,128)S(1)}, u32[]{:S(2)}, u32[]{:S(2)}) collective-permute-start(f32[8,64,128]{2,1,0:T(8,128)S(1)} %get-tuple-element.23.refs_0_), channel_id=1, source_target_pairs={{0,3},{1,2},{2,1},{3,0},{4,7},{5,6},{6,5},{7,4},{8,11},{9,10},{10,... | collective-permute-start | bytes 786440 | tf_op jit(solution)/shard_map/ppermute | solution.py:453
  90.4 3.9 %collective-permute-start.19 = (f32[2,8,16,128]{3,2,1,0:T(8,128)S(1)}, f32[2,8,16,128]{3,2,1,0:T(8,128)S(1)}, u32[]{:S(2)}, u32[]{:S(2)}) collective-permute-start(f32[2,8,16,128]{3,2,1,0:T(8,128)S(1)} %get-tuple-element.28), channel_id=1, source_target_pairs={{0,12},{4,16},{8,20},{12,24},{16,28},{20,32},{24,36},{28,40},{32,4... | collective-permute-start | bytes 393224 | tf_op jit(solution)/shard_map/ppermute | solution.py:486
  94.3 2.2 %collective-permute-start.20 = (f32[2,8,16,128]{3,2,1,0:T(8,128)S(1)}, f32[2,8,16,128]{3,2,1,0:T(8,128)S(1)}, u32[]{:S(2)}, u32[]{:S(2)}) collective-permute-start(f32[2,8,16,128]{3,2,1,0:T(8,128)S(1)} %get-tuple-element.29), channel_id=1, source_target_pairs={{0,16},{4,20},{8,24},{12,28},{16,32},{20,36},{24,40},{28,44},{32,4... | collective-permute-start | bytes 393224 | tf_op jit(solution)/shard_map/ppermute | solution.py:486
  96.6 3.6 %collective-permute-done.18.refs_2_ = f32[2,8,16,128]{3,2,1,0:T(8,128)S(1)} collective-permute-done((f32[2,8,16,128]{3,2,1,0:T(8,128)S(1)}, f32[2,8,16,128]{3,2,1,0:T(8,128)S(1)}, u32[]{:S(2)}, u32[]{:S(2)}) %collective-permute-start.18) | collective-permute-done | bytes 131104 | tf_op jit(solution)/shard_map/ppermute | solution.py:486
  100.1 11.4 %collective-permute-done.19.refs_3_ = f32[2,8,16,128]{3,2,1,0:T(8,128)S(1)} collective-permute-done((f32[2,8,16,128]{3,2,1,0:T(8,128)S(1)}, f32[2,8,16,128]{3,2,1,0:T(8,128)S(1)}, u32[]{:S(2)}, u32[]{:S(2)}) %collective-permute-start.19) | collective-permute-done | bytes 131104 | tf_op jit(solution)/shard_map/ppermute | solution.py:486
  112.8 2.7 %deposit.1 = (f32[8,4608]{1,0:T(8,128)S(1)}, f32[8,4608]{1,0:T(8,128)S(1)}) custom-call(s32[384]{0:T(512)S(1)} %reshape.10.refs_1_.offsets, f32[2,8,16,128]{3,2,1,0:T(8,128)S(1)} %get-tuple-element.25.refs_0_, f32[2,8,16,128]{3,2,1,0:T(8,128)S(1)} %collective-permute-done.17.refs_1_, f32[2,8,16,128]{3,2,1,0:T(8,128)S(1)} %collective-permute-done.18.refs_2_, ...), custom_call_target="tpu_custom_call" | custom-call | flops 8000000 | bytes 2097152 | tf_op jit(solution)/shard_map/deposit/pallas_call | solution.py:391
  115.5 2.2 %collective-permute-start.23 = (f32[8,4608]{1,0:T(8,128)S(1)}, f32[8,4608]{1,0:T(8,128)S(1)}, u32[]{:S(2)}, u32[]{:S(2)}) collective-permute-start(f32[8,4608]{1,0:T(8,128)S(1)} %get-tuple-element.30.refs_0_), channel_id=1, source_target_pairs={{0,3},{1,2},{2,1},{3,0},{4,7},{5,6},{6,5},{7,4},{8,11},{9,10},{10,... | collective-permute-start | bytes 442376 | tf_op jit(solution)/shard_map/ppermute | solution.py:453
  120.2 3.3 %collective-permute-done.23.refs_4_ = f32[8,4608]{1,0:T(8,128)S(1)} collective-permute-done((f32[8,4608]{1,0:T(8,128)S(1)}, f32[8,4608]{1,0:T(8,128)S(1)}, u32[]{:S(2)}, u32[]{:S(2)}) %collective-permute-start.23) | collective-permute-done | bytes 147488 | tf_op jit(solution)/shard_map/ppermute | solution.py:453
  123.5 2.0 %collective-permute-start.11 = (f32[8,64,128]{2,1,0:T(8,128)S(1)}, f32[8,64,128]{2,1,0:T(8,128)S(1)}, u32[]{:S(2)}, u32[]{:S(2)}) collective-permute-start(f32[8,64,128]{2,1,0:T(8,128)S(1)} %get-tuple-element.23.refs_0_), channel_id=1, source_target_pairs={{0,1},{1,0},{2,3},{3,2},{4,5},{5,4},{6,7},{7,6},{8,9},{9,8},{10,11... | collective-permute-start | bytes 786440 | tf_op jit(solution)/shard_map/ppermute | solution.py:453
  125.5 2.1 %collective-permute-start.14 = (f32[8,64,128]{2,1,0:T(8,128)S(1)}, f32[8,64,128]{2,1,0:T(8,128)S(1)}, u32[]{:S(2)}, u32[]{:S(2)}) collective-permute-start(f32[8,64,128]{2,1,0:T(8,128)S(1)} %get-tuple-element.24.refs_1_), channel_id=1, source_target_pairs={{0,3},{1,2},{2,1},{3,0},{4,7},{5,6},{6,5},{7,4},{8,11},{9,10},{10,... | collective-permute-start | bytes 786440 | tf_op jit(solution)/shard_map/ppermute | solution.py:453
  128.9 1.9 %collective-permute-done.25.refs_6_ = f32[8,4608]{1,0:T(8,128)S(1)} collective-permute-done((f32[8,4608]{1,0:T(8,128)S(1)}, f32[8,4608]{1,0:T(8,128)S(1)}, u32[]{:S(2)}, u32[]{:S(2)}) %collective-permute-start.25) | collective-permute-done | bytes 147488 | tf_op jit(solution)/shard_map/ppermute | solution.py:453
  130.7 1.6 %collective-permute-start.26 = (f32[8,4608]{1,0:T(8,128)S(1)}, f32[8,4608]{1,0:T(8,128)S(1)}, u32[]{:S(2)}, u32[]{:S(2)}) collective-permute-start(f32[8,4608]{1,0:T(8,128)S(1)} %collective-permute-done.22.refs_3_), channel_id=1, source_target_pairs={{0,3},{1,2},{2,1},{3,0},{4,7},{5,6},{6,5},{7,4},{8,11},{9,10},{10,... | collective-permute-start | bytes 442376 | tf_op jit(solution)/shard_map/ppermute | solution.py:453
  132.3 10.3 %collective-permute-done.26.refs_7_ = f32[8,4608]{1,0:T(8,128)S(1)} collective-permute-done((f32[8,4608]{1,0:T(8,128)S(1)}, f32[8,4608]{1,0:T(8,128)S(1)}, u32[]{:S(2)}, u32[]{:S(2)}) %collective-permute-start.26) | collective-permute-done | bytes 147488 | tf_op jit(solution)/shard_map/ppermute | solution.py:453
  (48 shorter events, 17.3 us)
Async XLA Ops:
  0.6 40.2 %collective-permute-start.6 = (f32[2,64,4096]{2,1,0:T(8,128)}, f32[2,64,4096]{2,1,0:T(8,128)}, u32[]{:S(2)}, u32[]{:S(2)}) collective-permute-start(f32[2,64,4096]{2,1,0:T(8,128)} %boxes.1), channel_id=1, source_target_pairs={{0,4},{4,0},{8,12},{12,8},{16,20},{20,16},{24,28},{28,24},{32,36},... | collective-permute-start | bytes 6291464 | tf_op jit(solution)/shard_map/ppermute | solution.py:471
  0.7 54.1 %collective-permute-start.5 = (f32[2,64,4096]{2,1,0:T(8,128)}, f32[2,64,4096]{2,1,0:T(8,128)}, u32[]{:S(2)}, u32[]{:S(2)}) collective-permute-start(f32[2,64,4096]{2,1,0:T(8,128)} %boxes.1), channel_id=1, source_target_pairs={{4,8},{8,4},{12,16},{16,12},{20,24},{24,20},{28,32},{32,28},{36,40... | collective-permute-start | bytes 6291464 | tf_op jit(solution)/shard_map/ppermute | solution.py:472
  9.3 23.3 %collective-permute-start.1 = (s32[12]{0:T(128)S(1)}, s32[12]{0:T(128)S(1)}, u32[]{:S(2)}, u32[]{:S(2)}) collective-permute-start(s32[12]{0:T(128)S(1)} %reshape.11), channel_id=1, source_target_pairs={{4,8},{8,4},{12,16},{16,12},{20,24},{24,20},{28,32},{32,28},{36,40... | collective-permute-start | bytes 152 | tf_op jit(solution)/shard_map/ppermute | solution.py:470
  11.2 21.3 %collective-permute-start = (s32[12]{0:T(128)S(1)}, s32[12]{0:T(128)S(1)}, u32[]{:S(2)}, u32[]{:S(2)}) collective-permute-start(s32[12]{0:T(128)S(1)} %reshape.11), channel_id=1, source_target_pairs={{0,4},{4,0},{8,12},{12,8},{16,20},{20,16},{24,28},{28,24},{32,36},... | collective-permute-start | bytes 152 | tf_op jit(solution)/shard_map/ppermute | solution.py:469
  63.6 10.9 %collective-permute-start.7 = (f32[16,64,128]{2,1,0:T(8,128)S(1)}, f32[16,64,128]{2,1,0:T(8,128)S(1)}, u32[]{:S(2)}, u32[]{:S(2)}) collective-permute-start(f32[16,64,128]{2,1,0:T(8,128)S(1)} %get-tuple-element.20), channel_id=1, source_target_pairs={{0,1},{1,0},{2,3},{3,2},{4,5},{5,4},{6,7},{7,6},{8,9},{9,8},{10,11... | collective-permute-start | bytes 1572872 | tf_op jit(solution)/shard_map/ppermute | solution.py:453
  63.9 13.9 %collective-permute-start.9 = (f32[16,64,128]{2,1,0:T(8,128)S(1)}, f32[16,64,128]{2,1,0:T(8,128)S(1)}, u32[]{:S(2)}, u32[]{:S(2)}) collective-permute-start(f32[16,64,128]{2,1,0:T(8,128)S(1)} %get-tuple-element.22), channel_id=1, source_target_pairs={{0,3},{1,2},{2,1},{3,0},{4,7},{5,6},{6,5},{7,4},{8,11},{9,10},{10,... | collective-permute-start | bytes 1572872 | tf_op jit(solution)/shard_map/ppermute | solution.py:453
  74.6 9.9 %collective-permute-start.8 = (f32[8,64,128]{2,1,0:T(8,128)S(1)}, f32[8,64,128]{2,1,0:T(8,128)S(1)}, u32[]{:S(2)}, u32[]{:S(2)}) collective-permute-start(f32[8,64,128]{2,1,0:T(8,128)S(1)} %slice_add_fusion.1), channel_id=1, source_target_pairs={{0,3},{1,2},{2,1},{3,0},{4,7},{5,6},{6,5},{7,4},{8,11},{9,10},{10,... | collective-permute-start | bytes 786440 | tf_op jit(solution)/shard_map/ppermute | solution.py:453
  77.9 7.4 %collective-permute-start.10 = (f32[8,64,128]{2,1,0:T(8,128)S(1)}, f32[8,64,128]{2,1,0:T(8,128)S(1)}, u32[]{:S(2)}, u32[]{:S(2)}) collective-permute-start(f32[8,64,128]{2,1,0:T(8,128)S(1)} %slice_add_fusion), channel_id=1, source_target_pairs={{0,1},{1,0},{2,3},{3,2},{4,5},{5,4},{6,7},{7,6},{8,9},{9,8},{10,11... | collective-permute-start | bytes 786440 | tf_op jit(solution)/shard_map/ppermute | solution.py:453
  86.0 32.8 %collective-permute-start.13 = (f32[8,64,128]{2,1,0:T(8,128)S(1)}, f32[8,64,128]{2,1,0:T(8,128)S(1)}, u32[]{:S(2)}, u32[]{:S(2)}) collective-permute-start(f32[8,64,128]{2,1,0:T(8,128)S(1)} %get-tuple-element.23.refs_0_), channel_id=1, source_target_pairs={{0,3},{1,2},{2,1},{3,0},{4,7},{5,6},{6,5},{7,4},{8,11},{9,10},{10,... | collective-permute-start | bytes 786440 | tf_op jit(solution)/shard_map/ppermute | solution.py:453
  88.9 7.6 %collective-permute-start.17 = (f32[2,8,16,128]{3,2,1,0:T(8,128)S(1)}, f32[2,8,16,128]{3,2,1,0:T(8,128)S(1)}, u32[]{:S(2)}, u32[]{:S(2)}) collective-permute-start(f32[2,8,16,128]{3,2,1,0:T(8,128)S(1)} %get-tuple-element.26), channel_id=1, source_target_pairs={{0,4},{4,8},{8,12},{12,16},{16,20},{20,24},{24,28},{28,32},{32,36}... | collective-permute-start | bytes 393224 | tf_op jit(solution)/shard_map/ppermute | solution.py:486
  89.0 11.2 %collective-permute-start.18 = (f32[2,8,16,128]{3,2,1,0:T(8,128)S(1)}, f32[2,8,16,128]{3,2,1,0:T(8,128)S(1)}, u32[]{:S(2)}, u32[]{:S(2)}) collective-permute-start(f32[2,8,16,128]{3,2,1,0:T(8,128)S(1)} %get-tuple-element.27), channel_id=1, source_target_pairs={{0,8},{4,12},{8,16},{12,20},{16,24},{20,28},{24,32},{28,36},{32,40... | collective-permute-start | bytes 393224 | tf_op jit(solution)/shard_map/ppermute | solution.py:486
  90.4 21.1 %collective-permute-start.19 = (f32[2,8,16,128]{3,2,1,0:T(8,128)S(1)}, f32[2,8,16,128]{3,2,1,0:T(8,128)S(1)}, u32[]{:S(2)}, u32[]{:S(2)}) collective-permute-start(f32[2,8,16,128]{3,2,1,0:T(8,128)S(1)} %get-tuple-element.28), channel_id=1, source_target_pairs={{0,12},{4,16},{8,20},{12,24},{16,28},{20,32},{24,36},{28,40},{32,4... | collective-permute-start | bytes 393224 | tf_op jit(solution)/shard_map/ppermute | solution.py:486
  94.3 18.5 %collective-permute-start.20 = (f32[2,8,16,128]{3,2,1,0:T(8,128)S(1)}, f32[2,8,16,128]{3,2,1,0:T(8,128)S(1)}, u32[]{:S(2)}, u32[]{:S(2)}) collective-permute-start(f32[2,8,16,128]{3,2,1,0:T(8,128)S(1)} %get-tuple-element.29), channel_id=1, source_target_pairs={{0,16},{4,20},{8,24},{12,28},{16,32},{20,36},{24,40},{28,44},{32,4... | collective-permute-start | bytes 393224 | tf_op jit(solution)/shard_map/ppermute | solution.py:486
  96.5 27.0 %collective-permute-start.12 = (f32[8,64,128]{2,1,0:T(8,128)S(1)}, f32[8,64,128]{2,1,0:T(8,128)S(1)}, u32[]{:S(2)}, u32[]{:S(2)}) collective-permute-start(f32[8,64,128]{2,1,0:T(8,128)S(1)} %get-tuple-element.24.refs_1_), channel_id=1, source_target_pairs={{0,1},{1,0},{2,3},{3,2},{4,5},{5,4},{6,7},{7,6},{8,9},{9,8},{10,11... | collective-permute-start | bytes 786440 | tf_op jit(solution)/shard_map/ppermute | solution.py:453
  115.5 8.0 %collective-permute-start.23 = (f32[8,4608]{1,0:T(8,128)S(1)}, f32[8,4608]{1,0:T(8,128)S(1)}, u32[]{:S(2)}, u32[]{:S(2)}) collective-permute-start(f32[8,4608]{1,0:T(8,128)S(1)} %get-tuple-element.30.refs_0_), channel_id=1, source_target_pairs={{0,3},{1,2},{2,1},{3,0},{4,7},{5,6},{6,5},{7,4},{8,11},{9,10},{10,... | collective-permute-start | bytes 442376 | tf_op jit(solution)/shard_map/ppermute | solution.py:453
  117.7 7.9 %collective-permute-start.21 = (f32[8,4608]{1,0:T(8,128)S(1)}, f32[8,4608]{1,0:T(8,128)S(1)}, u32[]{:S(2)}, u32[]{:S(2)}) collective-permute-start(f32[8,4608]{1,0:T(8,128)S(1)} %get-tuple-element.30.refs_0_), channel_id=1, source_target_pairs={{0,1},{1,0},{2,3},{3,2},{4,5},{5,4},{6,7},{7,6},{8,9},{9,8},{10,11... | collective-permute-start | bytes 442376 | tf_op jit(solution)/shard_map/ppermute | solution.py:453
  117.7 10.0 %collective-permute-start.24 = (f32[8,4608]{1,0:T(8,128)S(1)}, f32[8,4608]{1,0:T(8,128)S(1)}, u32[]{:S(2)}, u32[]{:S(2)}) collective-permute-start(f32[8,4608]{1,0:T(8,128)S(1)} %get-tuple-element.31.refs_1_), channel_id=1, source_target_pairs={{0,3},{1,2},{2,1},{3,0},{4,7},{5,6},{6,5},{7,4},{8,11},{9,10},{10,... | collective-permute-start | bytes 442376 | tf_op jit(solution)/shard_map/ppermute | solution.py:453
  118.8 8.8 %collective-permute-start.22 = (f32[8,4608]{1,0:T(8,128)S(1)}, f32[8,4608]{1,0:T(8,128)S(1)}, u32[]{:S(2)}, u32[]{:S(2)}) collective-permute-start(f32[8,4608]{1,0:T(8,128)S(1)} %get-tuple-element.31.refs_1_), channel_id=1, source_target_pairs={{0,1},{1,0},{2,3},{3,2},{4,5},{5,4},{6,7},{7,6},{8,9},{9,8},{10,11... | collective-permute-start | bytes 442376 | tf_op jit(solution)/shard_map/ppermute | solution.py:453
  123.5 7.2 %collective-permute-start.25 = (f32[8,4608]{1,0:T(8,128)S(1)}, f32[8,4608]{1,0:T(8,128)S(1)}, u32[]{:S(2)}, u32[]{:S(2)}) collective-permute-start(f32[8,4608]{1,0:T(8,128)S(1)} %collective-permute-done.23.refs_4_), channel_id=1, source_target_pairs={{0,1},{1,0},{2,3},{3,2},{4,5},{5,4},{6,7},{7,6},{8,9},{9,8},{10,11... | collective-permute-start | bytes 442376 | tf_op jit(solution)/shard_map/ppermute | solution.py:453
  123.5 20.1 %collective-permute-start.11 = (f32[8,64,128]{2,1,0:T(8,128)S(1)}, f32[8,64,128]{2,1,0:T(8,128)S(1)}, u32[]{:S(2)}, u32[]{:S(2)}) collective-permute-start(f32[8,64,128]{2,1,0:T(8,128)S(1)} %get-tuple-element.23.refs_0_), channel_id=1, source_target_pairs={{0,1},{1,0},{2,3},{3,2},{4,5},{5,4},{6,7},{7,6},{8,9},{9,8},{10,11... | collective-permute-start | bytes 786440 | tf_op jit(solution)/shard_map/ppermute | solution.py:453
  125.5 18.1 %collective-permute-start.14 = (f32[8,64,128]{2,1,0:T(8,128)S(1)}, f32[8,64,128]{2,1,0:T(8,128)S(1)}, u32[]{:S(2)}, u32[]{:S(2)}) collective-permute-start(f32[8,64,128]{2,1,0:T(8,128)S(1)} %get-tuple-element.24.refs_1_), channel_id=1, source_target_pairs={{0,3},{1,2},{2,1},{3,0},{4,7},{5,6},{6,5},{7,4},{8,11},{9,10},{10,... | collective-permute-start | bytes 786440 | tf_op jit(solution)/shard_map/ppermute | solution.py:453
  127.7 16.0 %collective-permute-start.15 = (f32[8,64,128]{2,1,0:T(8,128)S(1)}, f32[8,64,128]{2,1,0:T(8,128)S(1)}, u32[]{:S(2)}, u32[]{:S(2)}) collective-permute-start(f32[8,64,128]{2,1,0:T(8,128)S(1)} %collective-permute-done.13.refs_4_), channel_id=1, source_target_pairs={{0,1},{1,0},{2,3},{3,2},{4,5},{5,4},{6,7},{7,6},{8,9},{9,8},{10,11... | collective-permute-start | bytes 786440 | tf_op jit(solution)/shard_map/ppermute | solution.py:453
  127.7 16.0 %collective-permute-start.16 = (f32[8,64,128]{2,1,0:T(8,128)S(1)}, f32[8,64,128]{2,1,0:T(8,128)S(1)}, u32[]{:S(2)}, u32[]{:S(2)}) collective-permute-start(f32[8,64,128]{2,1,0:T(8,128)S(1)} %collective-permute-done.12.refs_3_), channel_id=1, source_target_pairs={{0,3},{1,2},{2,1},{3,0},{4,7},{5,6},{6,5},{7,4},{8,11},{9,10},{10,... | collective-permute-start | bytes 786440 | tf_op jit(solution)/shard_map/ppermute | solution.py:453
  130.7 11.9 %collective-permute-start.26 = (f32[8,4608]{1,0:T(8,128)S(1)}, f32[8,4608]{1,0:T(8,128)S(1)}, u32[]{:S(2)}, u32[]{:S(2)}) collective-permute-start(f32[8,4608]{1,0:T(8,128)S(1)} %collective-permute-done.22.refs_3_), channel_id=1, source_target_pairs={{0,3},{1,2},{2,1},{3,0},{4,7},{5,6},{6,5},{7,4},{8,11},{9,10},{10,... | collective-permute-start | bytes 442376 | tf_op jit(solution)/shard_map/ppermute | solution.py:453
  (5 other events, 42.8 us)

commit v2 on v1

--- a/solution.py
+++ b/solution.py
@@ -19,6 +19,8 @@
 FRONT = 16
 GROUP = 16
 ROOM = 32
+HALF = COLS // 8
+SIDES = (1, 3)
 QUARTER = COLS // 4
 SLABS = BOX // SLAB + 1
 SPAN = WIDE * BOX // 4 + 32 * WIDE
@@ -119,15 +121,15 @@
                 fresh = fresh - coupling[k - 1] * basis[k - 2, c + 1, pl.ds(8, BOX), :]
             return fresh
 
-        def group(start, carry, final):
+        def group(m, carry):
             norm, cross = carry
-            center = field[start + 1, pl.ds(8, BOX), :]
-            values = [center]
+            start = m * GROUP
+            values = [field[start + 1, pl.ds(8, BOX), :]]
             for u in range(1, GROUP + 1):
-                if final and u == GROUP:
-                    values.append(jnp.zeros_like(center))
-                    continue
-                fresh = value_of(start + u)
+                if u < GROUP:
+                    fresh = value_of(start + u)
+                else:
+                    fresh = jnp.where(start + u < COLS, value_of(jnp.minimum(start + u, COLS - 1)), 0.0)
                 field[start + u + 1, pl.ds(8, BOX), :] = fresh
                 norm = norm + fold(fresh * fresh)
                 values.append(fresh)
@@ -141,8 +143,7 @@
         opening = value_of(0)
         field[1, pl.ds(8, BOX), :] = opening
         carry = (fold(opening * opening), jnp.zeros((8, LANES), jnp.float32))
-        carry = lax.fori_loop(0, COLS // GROUP - 1, lambda m, held: group(m * GROUP, held, False), carry)
-        norm, cross = group(COLS - GROUP, carry, True)
+        norm, cross = lax.fori_loop(0, COLS // GROUP, group, carry)
         norm = total(norm)
         diagonal.append(total(cross) / norm)
         coupling.append(norm / norm_before if k > 0 else None)
@@ -159,9 +160,11 @@
     return weights
 
 
-def run_pair(own, other, first, second, delta, to_second, to_first, within, forces, *scratch):
+def run_pair(boxes, targets, within, forces, *scratch):
     buffer, still, shifted, basis, image = scratch
-    weights = solve_pair(own, other, first, second, delta, within, *scratch)
+    delta = boxes[4]
+    first, second, to_first, to_second = targets
+    weights = solve_pair(*boxes, within, *scratch)
 
     def finish(c, carry):
         potential = weights[0] * basis[0, c + 1, pl.ds(8, BOX), :]
@@ -192,16 +195,20 @@
         lax.fori_loop(0, COLS, deposit, 0, unroll=8)
 
 
-def pairs_kernel(begun, *refs):
+def pairs_kernel(phase, faraway, held, *refs):
+    begun = phase > 0 or faraway
+    lists, offsets, own, other_far, within, *refs = refs
     if begun:
-        lists, offsets, own, other_far, within, tally, forces_in, *parts, forces = refs[:12]
-    else:
-        lists, offsets, own, other_far, within, forces, tally_out = refs[:7]
+        tally, forces_in, *refs = refs
     other, other_sem, *scratch = refs[-7:]
     buffer, basis = scratch[0], scratch[3]
+    if faraway:
+        *parts, tally_out, forces = refs[:6]
+    else:
+        forces, tally_out = refs[:2]
     group, mine = place()
     near, far = neighbours(group)
-    neighbour, which = (far, 2) if begun else (near, 1)
+    neighbour, which = (far, 2) if faraway else (near, 1)
     copy = pltpu.make_async_copy(other_far, other, other_sem)
     copy.start()
 
@@ -222,8 +229,11 @@
         lax.fori_loop(0, COLS, clear_ends, 0, unroll=4)
 
     def open_forces(c, carry):
-        for k in range(2):
-            forces[k, c] = forces_in[k, c] if begun else jnp.zeros((BOX, LANES), jnp.float32)
+        for k in held:
+            block = jnp.zeros((BOX, LANES), jnp.float32)
+            if begun:
+                block = forces_in[k if forces_in.shape[0] > 1 else 0, c]
+            forces[k - held[0], c] = block
         return carry
 
     lax.fori_loop(0, COLS, open_forces, 0, unroll=2)
@@ -239,31 +249,38 @@
         second_group = second >> 1
         inner = second_group == group
         outer = second_group == neighbour
-        if begun:
+        second_at = second - 2 * group
+        first_at = first - 2 * group
+        if faraway:
             wanted = jnp.where(foreign > 0, inner, outer)
         else:
             wanted = jnp.where(foreign > 0, inner, inner | outer)
-        taken = live & wanted
+        if phase == 0:
+            timely = ((foreign == 0) & (first_at == 0)) | (inner & (second_at == 0))
+        else:
+            timely = ((foreign > 0) | (first_at == 1)) & (jnp.logical_not(inner) | (second_at == 1))
+        taken = live & wanted & timely
         turn = taken & ((count & 3) == mine)
 
         @pl.when(turn)
         def _():
             delta = [offsets[first * 3 + axis] - offsets[second * 3 + axis] for axis in range(3)]
-            first_at = jnp.where(foreign > 0, 2 + first - 2 * neighbour, first - 2 * group)
-            second_at = jnp.where(inner, second - 2 * group, 2 + second - 2 * neighbour)
-            run_pair(own, other, first_at, second_at, delta, inner, foreign == 0, within, forces, *scratch)
+            first_box = jnp.where(foreign > 0, 2 + first - 2 * neighbour, first_at)
+            second_box = jnp.where(inner, second_at, 2 + second - 2 * neighbour)
+            boxes = (own, other, first_box, second_box, delta)
+            targets = (first_at - held[0], second_at - held[0], foreign == 0, inner)
+            run_pair(boxes, targets, within, forces, *scratch)
 
         return count + taken.astype(jnp.int32)
 
-    if not begun:
-        tally_out[0] = lax.fori_loop(0, 32, slot, jnp.int32(0))
+    tally_out[0] = lax.fori_loop(0, 32, slot, tally[0] if begun else jnp.int32(0))
+    if not faraway:
         return
-    lax.fori_loop(0, 32, slot, tally[0])
-    for k, side in enumerate((1, 3)):
+    for h, side in enumerate(SIDES):
         for n, who in enumerate((mine ^ side, mine)):
-            for half, quarter in enumerate((who, who ^ (4 - side))):
-                for c in range(QUARTER):
-                    parts[2 * k + n][half * QUARTER + c] = forces[k, quarter * QUARTER + c]
+            for m, quarter in enumerate((who, who ^ (4 - side))):
+                for c in range(HALF):
+                    parts[2 * h + n][m * HALF + c] = forces[0, quarter * QUARTER + h * HALF + c]
 
 
 def within_block():
@@ -290,98 +307,106 @@
     )(boxes)
 
 
-def run_pairs(lists, offsets, own, other, before=None):
-    begun = before is not None
+def run_pairs(lists, offsets, own, other, phase, faraway, tally=None, forces=None):
     operands = [lists, offsets, own, other, within_block()]
     in_specs = [SMEM, SMEM, VMEM, HBM, VMEM]
-    whole = (2, COLS, BOX, LANES)
+    held = (0, 1) if tally is None else (phase,)
+    whole = (len(held), COLS, BOX, LANES)
     scratch = [
         pltpu.VMEM((2, BOX, BOX * BOX), jnp.float32),
         pltpu.SemaphoreType.DMA,
         pltpu.VMEM((COLS + 2 * FRONT, BOX + 2 * ROOM, LANES), jnp.float32),
         pltpu.VMEM((COLS, BOX, LANES), jnp.float32),
         pltpu.VMEM((COLS, BOX, LANES), jnp.float32),
-        pltpu.VMEM((ITERS, COLS + 1, BOX + 16, LANES), jnp.float32),
+        pltpu.VMEM((ITERS, COLS + 2, BOX + 16, LANES), jnp.float32),
         pltpu.VMEM((COLS, BOX, LANES), jnp.float32),
     ]
-    if begun:
-        operands += [before[1], before[0]]
+    if tally is not None:
+        operands += [tally, forces]
         in_specs += [SMEM, VMEM]
-        out_shape = [jax.ShapeDtypeStruct((2 * QUARTER, BOX, LANES), jnp.float32)] * 4
-        out_specs = [VMEM] * 4
+    counted = jax.ShapeDtypeStruct((1,), jnp.int32)
+    if faraway:
+        out_shape = [jax.ShapeDtypeStruct((2 * HALF, BOX, LANES), jnp.float32)] * 4 + [counted]
+        out_specs = [VMEM] * 4 + [SMEM]
         scratch = [pltpu.VMEM(whole, jnp.float32)] + scratch
     else:
-        out_shape = [jax.ShapeDtypeStruct(whole, jnp.float32), jax.ShapeDtypeStruct((1,), jnp.int32)]
+        out_shape = [jax.ShapeDtypeStruct(whole, jnp.float32), counted]
         out_specs = [VMEM, SMEM]
     return pl.pallas_call(
-        functools.partial(pairs_kernel, begun),
+        functools.partial(pairs_kernel, phase, faraway, held),
         out_shape=out_shape,
         in_specs=in_specs,
         out_specs=out_specs,
         scratch_shapes=scratch,
         compiler_params=pltpu.CompilerParams(vmem_limit_bytes=PAIRS_VMEM),
         cost_estimate=pl.CostEstimate(flops=100_000_000, bytes_accessed=8 << 20, transcendentals=0),
-        name="pairs_far" if begun else "pairs_near",
     )(*operands)
 
 
-def settle_kernel(offsets, *refs):
-    parts, sums, pieces, tall = refs[:6], refs[6:8], refs[8:13], refs[13]
+def settle_kernel(phase, offsets, *refs):
+    parts, refs = refs[:6], refs[6:]
+    if phase > 0:
+        earlier, refs = refs[:2], refs[2:]
+    sums, pieces, tall = refs[:2], refs[2 : 2 + SLABS], refs[-1]
     group, _ = place()
-    for k in range(2):
-        kept, once, twice = parts[3 * k : 3 * k + 3]
-        tall[:, pl.ds(0, SLAB), :] = jnp.zeros((QUARTER, SLAB, LANES), jnp.float32)
-        tall[:, pl.ds(SLAB + BOX, SLAB), :] = jnp.zeros((QUARTER, SLAB, LANES), jnp.float32)
+    tall[:, pl.ds(0, SLAB), :] = jnp.zeros((QUARTER, SLAB, LANES), jnp.float32)
+    tall[:, pl.ds(SLAB + BOX, SLAB), :] = jnp.zeros((QUARTER, SLAB, LANES), jnp.float32)
+    for h in range(2):
+        kept, once, twice = parts[3 * h : 3 * h + 3]
+        for c in range(HALF):
+            value = (kept[c] + once[c]) + twice[c]
+            if phase > 0:
+                sums[h][0, c] = earlier[h][0, c]
+            sums[h][phase, c] = value
+            tall[h * HALF + c, pl.ds(SLAB, BOX), :] = value
+    depth = offsets[(2 * group + phase) * 3] - group * SLAB
+    for t in range(SLABS):
         for c in range(QUARTER):
-            value = (kept[c] + once[c]) + twice[c]
-            sums[k][c] = value
-            tall[c, pl.ds(SLAB, BOX), :] = value
-        depth = offsets[(2 * group + k) * 3] - group * SLAB
-        for t in range(SLABS):
-            for c in range(QUARTER):
-                pieces[t][k, c] = tall[c, pl.ds(SLAB * (t + 1) - depth, SLAB), :]
-
-
-def settle(offsets, parts):
-    quarter = jax.ShapeDtypeStruct((QUARTER, BOX, LANES), jnp.float32)
-    piece = jax.ShapeDtypeStruct((2, QUARTER, SLAB, LANES), jnp.float32)
+            pieces[t][c] = tall[c, pl.ds(SLAB * (t + 1) - depth, SLAB), :]
+
+
+def settle(offsets, phase, parts, earlier=()):
+    half = jax.ShapeDtypeStruct((phase + 1, HALF, BOX, LANES), jnp.float32)
+    piece = jax.ShapeDtypeStruct((QUARTER, SLAB, LANES), jnp.float32)
     return pl.pallas_call(
-        settle_kernel,
-        out_shape=[quarter] * 2 + [piece] * SLABS,
-        in_specs=[SMEM] + [VMEM] * 6,
+        functools.partial(settle_kernel, phase),
+        out_shape=[half] * 2 + [piece] * SLABS,
+        in_specs=[SMEM] + [VMEM] * (6 + len(earlier)),
         out_specs=[VMEM] * (2 + SLABS),
         scratch_shapes=[pltpu.VMEM((QUARTER, BOX + 2 * SLAB, LANES), jnp.float32)],
+        compiler_params=pltpu.CompilerParams(vmem_limit_bytes=SMALL_VMEM),
         cost_estimate=pl.CostEstimate(flops=4_000_000, bytes_accessed=4 << 20, transcendentals=0),
-        compiler_params=pltpu.CompilerParams(vmem_limit_bytes=SMALL_VMEM),
-        name="settle",
-    )(offsets, *parts)
+    )(offsets, *parts, *earlier)
 
 
 def deposit_kernel(offsets, *refs):
-    pieces, outs, span = refs[:SLABS], refs[SLABS : SLABS + 2], refs[-1]
+    pieces, outs, table, span = refs[: 2 * SLABS], refs[2 * SLABS : 2 * SLABS + 2], refs[-2], refs[-1]
     group, _ = place()
+    groups = lax.axis_size("orb")
     lanes = lax.broadcasted_iota(jnp.int32, (SLAB, LANES), 1)
     span[...] = jnp.zeros_like(span)
-    for t in range(SLABS):
-        owner = (group + lax.axis_size("orb") - t) % lax.axis_size("orb")
-
-        def lay(k, carry):
-            at = (2 * owner + k) * 3
-            base = offsets[at + 1] * WIDE + offsets[at + 2]
-            for c in range(QUARTER):
-                value = pieces[t][k, c]
-                for row in range(2):
-                    start = base + (2 * c + row) * WIDE - row * BOX
-                    tile, turn = start >> 7, start & (LANES - 1)
-                    kept = (lanes < BOX) if row == 0 else (lanes >= BOX)
-                    turned = pltpu.roll(jnp.where(kept, value, 0.0), turn, 1)
-                    here = pl.ds(pl.multiple_of(tile * LANES, LANES), LANES)
-                    there = pl.ds(pl.multiple_of(tile * LANES + LANES, LANES), LANES)
-                    span[:, here] = span[:, here] + jnp.where(lanes >= turn, turned, 0.0)
-                    span[:, there] = span[:, there] + jnp.where(lanes < turn, turned, 0.0)
-            return carry
-
-        lax.fori_loop(0, 2, lay, 0)
+    for n in range(2 * SLABS):
+        table[n] = pieces[n][...]
+
+    def lay(n, carry):
+        k = (n >= SLABS).astype(jnp.int32)
+        owner = (group + groups - (n - k * SLABS)) & (groups - 1)
+        at = (2 * owner + k) * 3
+        base = offsets[at + 1] * WIDE + offsets[at + 2]
+        for c in range(QUARTER):
+            value = table[n, c]
+            for row in range(2):
+                start = base + (2 * c + row) * WIDE - row * BOX
+                tile, turn = start >> 7, start & (LANES - 1)
+                kept = (lanes < BOX) if row == 0 else (lanes >= BOX)
+                turned = pltpu.roll(jnp.where(kept, value, 0.0), turn, 1)
+                here = pl.ds(pl.multiple_of(tile * LANES, LANES), LANES)
+                there = pl.ds(pl.multiple_of(tile * LANES + LANES, LANES), LANES)
+                span[:, here] = span[:, here] + jnp.where(lanes >= turn, turned, 0.0)
+                span[:, there] = span[:, there] + jnp.where(lanes < turn, turned, 0.0)
+        return carry
+
+    lax.fori_loop(0, 2 * SLABS, lay, 0)
     for half in range(2):
         outs[half][...] = span[pl.ds(8 * half, 8), pl.ds(0, SPAN)]
 
@@ -391,9 +416,12 @@
     return pl.pallas_call(
         deposit_kernel,
         out_shape=[half] * 2,
-        in_specs=[SMEM] + [VMEM] * SLABS,
+        in_specs=[SMEM] + [VMEM] * (2 * SLABS),
         out_specs=[VMEM] * 2,
-        scratch_shapes=[pltpu.VMEM((SLAB, SPAN + 4 * LANES), jnp.float32)],
+        scratch_shapes=[
+            pltpu.VMEM((2 * SLABS, QUARTER, SLAB, LANES), jnp.float32),
+            pltpu.VMEM((SLAB, SPAN + 4 * LANES), jnp.float32),
+        ],
         cost_estimate=pl.CostEstimate(flops=8_000_000, bytes_accessed=2 << 20, transcendentals=0),
         compiler_params=pltpu.CompilerParams(vmem_limit_bytes=SMALL_VMEM),
         name="deposit",
@@ -431,10 +459,11 @@
     parts, out = refs[:8], refs[8]
     _, mine = place()
     for n, quarter in enumerate(quarters_of(mine)):
-        for k in range(2):
-            for c in range(QUARTER):
-                where = pl.ds(pl.multiple_of((quarter * QUARTER + c) * LANES, LANES), LANES)
-                out[k, :, where] = parts[2 * n + k][c]
+        for h in range(2):
+            for c in range(HALF):
+                where = pl.ds(pl.multiple_of((quarter * QUARTER + h * HALF + c) * LANES, LANES), LANES)
+                for k in range(2):
+                    out[k, :, where] = parts[2 * n + h][k, c]
 
 
 def assemble(parts):
@@ -459,6 +488,21 @@
     first_two = across(first_three, 1)
     second_two = across(second_one, 3)
     return [first, second, first_one, second_one, first_three, second_three, first_two, second_two]
+
+
+def reduce_scatter(parts):
+    sent, kept = parts[0::2], parts[1::2]
+    got = [across(sent[h], side) for h, side in enumerate(SIDES)]
+    passed = [kept[h][HALF:] + got[h][HALF:] for h in range(2)]
+    last = [across(passed[h], 4 - side) for h, side in enumerate(SIDES)]
+    return [kept[0], got[0], last[0], kept[1], got[1], last[1]]
+
+
+def deal(pieces, groups):
+    dealt = [pieces[0]]
+    for later in range(1, SLABS):
+        dealt.append(lax.ppermute(pieces[later], "orb", [(i, (i + later) % groups) for i in range(groups)]))
+    return dealt
 
 
 def shards(orbitals, pair_list, box_offsets):
@@ -474,16 +518,16 @@
     lists = jnp.concatenate([known] + [across(known, side) for side in (1, 2, 3)])
     offsets = box_offsets.reshape(-1)
     own = stage(orbitals)
-    before = run_pairs(lists, offsets, own, near)
-    sent_zero, kept_zero, sent_one, kept_one = run_pairs(lists, offsets, own, far, before)
-    got_zero, got_one = across(sent_zero, 1), across(sent_one, 3)
-    last_zero = across(kept_zero[QUARTER:] + got_zero[QUARTER:], 3)
-    last_one = across(kept_one[QUARTER:] + got_one[QUARTER:], 1)
-    settled = settle(offsets, (kept_zero, got_zero, last_zero, kept_one, got_one, last_one))
-    pieces = [settled[2]]
-    for later in range(1, SLABS):
-        route = [(i, (i + later) % groups) for i in range(groups)]
-        pieces.append(lax.ppermute(settled[2 + later], "orb", route))
+    shared, tally = run_pairs(lists, offsets, own, near, 0, False)
+    *parts, tally = run_pairs(lists, offsets, own, far, 0, True, tally, shared)
+    summed = reduce_scatter(parts)
+    shared, tally = run_pairs(lists, offsets, own, near, 1, False, tally, shared)
+    *parts, tally = run_pairs(lists, offsets, own, far, 1, True, tally, shared)
+    settled = settle(offsets, 0, summed)
+    pieces = deal(settled[2:], groups)
+    summed = reduce_scatter(parts)
+    settled = settle(offsets, 1, summed, settled[:2])
+    pieces += deal(settled[2:], groups)
     gathered = gather_pair(settled[0], settled[1])
     forces = assemble(gathered)
     spans = deposit(offsets, pieces)

time: 145 us -> 166 us (1.14)
  Pallas kernels: 28.7 us -> 37.2 us
  starting transfers between devices: 42.3 us -> 50.4 us
  waiting for transfers between devices: 69.8 us -> 73.4 us
    pallas_call x3 -> x6, Pallas kernels: 23.4 us -> 31.8 us  [the longest x4 30.5 us: run_pairs(): pl.pallas_call(functools.partial(pairs_kernel, phase, faraway, held), out...]
    ppermute x19 -> x23, starting transfers between devices: 24.8 us -> 31.9 us  [across(): lax.ppermute(block, 'rep', [(i, i ^ side) for i in range(lax.axis_size('r...]
    ppermute x4 -> x8, waiting for transfers between devices: 16.3 us -> 22.1 us  [deal(): lax.ppermute(pieces[later], 'orb', [(i, (i + later) % groups) for i in ra...]
    ppermute x19 -> x23, waiting for transfers between devices: 35.1 us -> 33.8 us  [across(): lax.ppermute(block, 'rep', [(i, i ^ side) for i in range(lax.axis_size('r...]
    ppermute x4 -> x8, starting transfers between devices: 7.59 us -> 7.63 us  [deal(): lax.ppermute(pieces[later], 'orb', [(i, (i + later) % groups) for i in ra...]
  transfers between devices with their start and end apart: 27 -> 35, of which waited for: 12 -> 15; matrix products, arithmetic and copies ran while one was open for 1% -> 1% of each run, Pallas kernels for 12% -> 17%
where the time goes in v2:
time: 166 us; the launch traced here: 165 us
  waiting for transfers between devices  73.4 us (44%)
  starting transfers between devices  50.4 us (30%)
  Pallas kernels  37.2 us (22%)
  local copies, waits for them, and re-layouts  3.43 us (2%)
    ppermute x23, waiting for transfers between devices, across(): lax.ppermute(block, 'rep', [(i, i ^ side) for i in range(lax.axis_size('r...  33.8 us
    ppermute x23, starting transfers between devices, across(): lax.ppermute(block, 'rep', [(i, i ^ side) for i in range(lax.axis_size('r...  31.9 us
    pallas_call x4, Pallas kernels, run_pairs(): pl.pallas_call(functools.partial(pairs_kernel, phase, faraway, held), out...  30.5 us
    ppermute x8, waiting for transfers between devices, deal(): lax.ppermute(pieces[later], 'orb', [(i, (i + later) % groups) for i in ra...  22.1 us
    ppermute x1, waiting for transfers between devices, shards(): far_slots = lax.ppermute(slots, 'orb', to_far)  17.5 us
    ppermute x1, starting transfers between devices, shards(): far = lax.ppermute(orbitals, 'orb', to_far)  7.83 us
    ppermute x8, starting transfers between devices, deal(): lax.ppermute(pieces[later], 'orb', [(i, (i + later) % groups) for i in ra...  7.63 us
  transfers between devices with their start and end apart: 35, of which 15 were waited for; matrix products, arithmetic and copies ran while one was open for 1% of the time, Pallas kernels for 17%

profile of v2, /device:TPU:4, one launch (start us, length us, event | category | flops | bytes accessed | tf_op | source)
XLA Modules:
  0.0 165.5 jit_solution(13139067838500196183)
XLA Ops:
  0.7 7.8 %collective-permute-start.5 = (f32[2,64,4096]{2,1,0:T(8,128)}, f32[2,64,4096]{2,1,0:T(8,128)}, u32[]{:S(2)}, u32[]{:S(2)}) collective-permute-start(f32[2,64,4096]{2,1,0:T(8,128)} %boxes.1), channel_id=1, source_target_pairs={{4,8},{8,4},{12,16},{16,12},{20,24},{24,20},{28,32},{32,28},{36,40... | collective-permute-start | bytes 6291464 | tf_op jit(solution)/shard_map/ppermute | solution.py:516
  9.3 3.0 %collective-permute-start.1 = (s32[12]{0:T(128)S(1)}, s32[12]{0:T(128)S(1)}, u32[]{:S(2)}, u32[]{:S(2)}) collective-permute-start(s32[12]{0:T(128)S(1)} %reshape.11), channel_id=1, source_target_pairs={{4,8},{8,4},{12,16},{16,12},{20,24},{24,20},{28,32},{32,28},{36,40... | collective-permute-start | bytes 152 | tf_op jit(solution)/shard_map/ppermute | solution.py:514
  15.1 17.5 %collective-permute-done.1 = s32[12]{0:T(128)S(1)} collective-permute-done((s32[12]{0:T(128)S(1)}, s32[12]{0:T(128)S(1)}, u32[]{:S(2)}, u32[]{:S(2)}) %collective-permute-start.1) | collective-permute-done | bytes 80 | tf_op jit(solution)/shard_map/ppermute | solution.py:514
  34.3 2.9 %collective-permute-start.3 = (s32[36]{0:T(128)S(1)}, s32[36]{0:T(128)S(1)}, u32[]{:S(2)}, u32[]{:S(2)}) collective-permute-start(s32[36]{0:T(128)S(1)} %pad_add_fusion), channel_id=1, source_target_pairs={{0,2},{1,3},{2,0},{3,1},{4,6},{5,7},{6,4},{7,5},{8,10},{9,11},{10,... | collective-permute-start | bytes 440 | tf_op jit(solution)/shard_map/ppermute | solution.py:482
  39.3 2.6 %collective-permute-done.4 = s32[36]{0:T(128)S(1)} collective-permute-done((s32[36]{0:T(128)S(1)}, s32[36]{0:T(128)S(1)}, u32[]{:S(2)}, u32[]{:S(2)}) %collective-permute-start.4) | collective-permute-done | bytes 176 | tf_op jit(solution)/shard_map/ppermute | solution.py:482
  42.0 14.3 %shard_map.86 = (f32[2,32,64,128]{3,2,1,0:T(8,128)S(1)}, s32[1]{0:T(128)}) custom-call(s32[144]{0:T(256)S(1)} %concatenate.8.refs_0_, s32[384]{0:T(512)S(1)} %reshape.10.refs_1_.offsets, f32[2,64,4096]{2,1,0:T(8,128)S(1)} %stage.1.refs_2_, f32[2,64,4096]{2,1,0:T(8,128)} %collective-permute-done.6.refs_3_, bf16[256,128]{1,0:T(8,128)(2,1)S(1)} %copy-done.1), custom_call_target="tpu_custom_call" | custom-call | flops 100000000 | bytes 8388608 | tf_op jit(solution)/shard_map/pallas_call | solution.py:335
  56.4 3.3 %shard_map.87 = (f32[8,64,128]{2,1,0:T(8,128)S(1)}, f32[8,64,128]{2,1,0:T(8,128)S(1)}, f32[8,64,128]{2,1,0:T(8,128)S(1)}, f32[8,64,128]{2,1,0:T(8,128)S(1)}, s32[1]{0:T(128)}) custom-call(s32[144]{0:T(256)S(1)} %concatenate.8.refs_0_, s32[384]{0:T(512)S(1)} %reshape.10.refs_1_.offsets, f32[2,64,4096]{2,1,0:T(8,128)S(1)} %stage.1.refs_2_, ...), custom_call_target="tpu_custom_call" | custom-call | flops 100000000 | bytes 8388608 | tf_op jit(solution)/shard_map/pallas_call | solution.py:335
  60.9 9.5 %shard_map.88 = (f32[1,32,64,128]{3,2,1,0:T(8,128)S(1)}, s32[1]{0:T(128)}) custom-call(s32[144]{0:T(256)S(1)} %concatenate.8.refs_0_, s32[384]{0:T(512)S(1)} %reshape.10.refs_1_.offsets, f32[2,64,4096]{2,1,0:T(8,128)S(1)} %stage.1.refs_2_, f32[2,64,4096]{2,1,0:T(8,128)} %collective-permute-done.6.refs_3_, bf16[256,128]{1,0:T(8,128)(2,1)S(1)} %copy-done.1, ...), custom_call_target="tpu_custom_call" | custom-call | flops 100000000 | bytes 8388608 | tf_op jit(solution)/shard_map/pallas_call | solution.py:335
  70.4 3.3 %shard_map.89 = (f32[8,64,128]{2,1,0:T(8,128)S(1)}, f32[8,64,128]{2,1,0:T(8,128)S(1)}, f32[8,64,128]{2,1,0:T(8,128)S(1)}, f32[8,64,128]{2,1,0:T(8,128)S(1)}, s32[1]{0:T(128)}) custom-call(s32[144]{0:T(256)S(1)} %concatenate.8.refs_0_, s32[384]{0:T(512)S(1)} %reshape.10.refs_1_.offsets, f32[2,64,4096]{2,1,0:T(8,128)S(1)} %stage.1.refs_2_, ...), custom_call_target="tpu_custom_call" | custom-call | flops 100000000 | bytes 8388608 | tf_op jit(solution)/shard_map/pallas_call | solution.py:335
  73.8 7.8 %collective-permute-start.9 = (f32[8,64,128]{2,1,0:T(8,128)S(1)}, f32[8,64,128]{2,1,0:T(8,128)S(1)}, u32[]{:S(2)}, u32[]{:S(2)}) collective-permute-start(f32[8,64,128]{2,1,0:T(8,128)S(1)} %get-tuple-element.39), channel_id=1, source_target_pairs={{0,3},{1,2},{2,1},{3,0},{4,7},{5,6},{6,5},{7,4},{8,11},{9,10},{10,... | collective-permute-start | bytes 786440 | tf_op jit(solution)/shard_map/ppermute | solution.py:482
  83.9 4.6 %collective-permute-done.9.refs_4_ = f32[8,64,128]{2,1,0:T(8,128)S(1)} collective-permute-done((f32[8,64,128]{2,1,0:T(8,128)S(1)}, f32[8,64,128]{2,1,0:T(8,128)S(1)}, u32[]{:S(2)}, u32[]{:S(2)}) %collective-permute-start.9) | collective-permute-done | bytes 262176 | tf_op jit(solution)/shard_map/ppermute | solution.py:482
  88.7 3.0 %collective-permute-start.8 = (f32[4,64,128]{2,1,0:T(8,128)S(1)}, f32[4,64,128]{2,1,0:T(8,128)S(1)}, u32[]{:S(2)}, u32[]{:S(2)}) collective-permute-start(f32[4,64,128]{2,1,0:T(8,128)S(1)} %slice_add_fusion.3), channel_id=1, source_target_pairs={{0,3},{1,2},{2,1},{3,0},{4,7},{5,6},{6,5},{7,4},{8,11},{9,10},{10,... | collective-permute-start | bytes 393224 | tf_op jit(solution)/shard_map/ppermute | solution.py:482
  92.3 2.6 %collective-permute-done.10.refs_5_ = f32[4,64,128]{2,1,0:T(8,128)S(1)} collective-permute-done((f32[4,64,128]{2,1,0:T(8,128)S(1)}, f32[4,64,128]{2,1,0:T(8,128)S(1)}, u32[]{:S(2)}, u32[]{:S(2)}) %collective-permute-start.10) | collective-permute-done | bytes 131104 | tf_op jit(solution)/shard_map/ppermute | solution.py:482
  98.1 5.3 %collective-permute-start.28 = (f32[8,16,128]{2,1,0:T(8,128)S(1)}, f32[8,16,128]{2,1,0:T(8,128)S(1)}, u32[]{:S(2)}, u32[]{:S(2)}) collective-permute-start(f32[8,16,128]{2,1,0:T(8,128)S(1)} %get-tuple-element.57), channel_id=1, source_target_pairs={{0,16},{4,20},{8,24},{12,28},{16,32},{20,36},{24,40},{28,44},{32,4... | collective-permute-start | bytes 196616 | tf_op jit(solution)/shard_map/ppermute | solution.py:504
  103.5 8.4 %collective-permute-done.26.refs_7_ = f32[8,16,128]{2,1,0:T(8,128)S(1)} collective-permute-done((f32[8,16,128]{2,1,0:T(8,128)S(1)}, f32[8,16,128]{2,1,0:T(8,128)S(1)}, u32[]{:S(2)}, u32[]{:S(2)}) %collective-permute-start.26) | collective-permute-done | bytes 65568 | tf_op jit(solution)/shard_map/ppermute | solution.py:504
  111.8 4.0 %collective-permute-done.27.refs_8_ = f32[8,16,128]{2,1,0:T(8,128)S(1)} collective-permute-done((f32[8,16,128]{2,1,0:T(8,128)S(1)}, f32[8,16,128]{2,1,0:T(8,128)S(1)}, u32[]{:S(2)}, u32[]{:S(2)}) %collective-permute-start.27) | collective-permute-done | bytes 65568 | tf_op jit(solution)/shard_map/ppermute | solution.py:504
  115.8 2.9 %collective-permute-done.28.refs_9_ = f32[8,16,128]{2,1,0:T(8,128)S(1)} collective-permute-done((f32[8,16,128]{2,1,0:T(8,128)S(1)}, f32[8,16,128]{2,1,0:T(8,128)S(1)}, u32[]{:S(2)}, u32[]{:S(2)}) %collective-permute-start.28) | collective-permute-done | bytes 65568 | tf_op jit(solution)/shard_map/ppermute | solution.py:504
  118.7 4.1 %collective-permute-done.23.refs_3_ = f32[8,16,128]{2,1,0:T(8,128)S(1)} collective-permute-done((f32[8,16,128]{2,1,0:T(8,128)S(1)}, f32[8,16,128]{2,1,0:T(8,128)S(1)}, u32[]{:S(2)}, u32[]{:S(2)}) %collective-permute-start.23) | collective-permute-done | bytes 65568 | tf_op jit(solution)/shard_map/ppermute | solution.py:504
  122.8 2.8 %collective-permute-done.24.refs_4_ = f32[8,16,128]{2,1,0:T(8,128)S(1)} collective-permute-done((f32[8,16,128]{2,1,0:T(8,128)S(1)}, f32[8,16,128]{2,1,0:T(8,128)S(1)}, u32[]{:S(2)}, u32[]{:S(2)}) %collective-permute-start.24) | collective-permute-done | bytes 65568 | tf_op jit(solution)/shard_map/ppermute | solution.py:504
  125.6 2.7 %deposit.1 = (f32[8,4608]{1,0:T(8,128)S(1)}, f32[8,4608]{1,0:T(8,128)S(1)}) custom-call(s32[384]{0:T(512)S(1)} %reshape.10.refs_1_.offsets, f32[8,16,128]{2,1,0:T(8,128)S(1)} %get-tuple-element.48.refs_0_, f32[8,16,128]{2,1,0:T(8,128)S(1)} %collective-permute-done.21.refs_1_, f32[8,16,128]{2,1,0:T(8,128)S(1)} %collective-permute-done.22.refs_2_, ...), custom_call_target="tpu_custom_call" | custom-call | flops 8000000 | bytes 2097152 | tf_op jit(solution)/shard_map/deposit/pallas_call | solution.py:416
  133.7 2.6 %collective-permute-done.31.refs_4_ = f32[8,4608]{1,0:T(8,128)S(1)} collective-permute-done((f32[8,4608]{1,0:T(8,128)S(1)}, f32[8,4608]{1,0:T(8,128)S(1)}, u32[]{:S(2)}, u32[]{:S(2)}) %collective-permute-start.31) | collective-permute-done | bytes 147488 | tf_op jit(solution)/shard_map/ppermute | solution.py:482
  137.7 6.3 %collective-permute-done.30.refs_3_ = f32[8,4608]{1,0:T(8,128)S(1)} collective-permute-done((f32[8,4608]{1,0:T(8,128)S(1)}, f32[8,4608]{1,0:T(8,128)S(1)}, u32[]{:S(2)}, u32[]{:S(2)}) %collective-permute-start.30) | collective-permute-done | bytes 147488 | tf_op jit(solution)/shard_map/ppermute | solution.py:482
  144.0 3.2 %collective-permute-done.29.refs_2_ = f32[8,4608]{1,0:T(8,128)S(1)} collective-permute-done((f32[8,4608]{1,0:T(8,128)S(1)}, f32[8,4608]{1,0:T(8,128)S(1)}, u32[]{:S(2)}, u32[]{:S(2)}) %collective-permute-start.29) | collective-permute-done | bytes 147488 | tf_op jit(solution)/shard_map/ppermute | solution.py:482
  153.2 9.7 %collective-permute-done.34.refs_7_ = f32[8,4608]{1,0:T(8,128)S(1)} collective-permute-done((f32[8,4608]{1,0:T(8,128)S(1)}, f32[8,4608]{1,0:T(8,128)S(1)}, u32[]{:S(2)}, u32[]{:S(2)}) %collective-permute-start.34) | collective-permute-done | bytes 147488 | tf_op jit(solution)/shard_map/ppermute | solution.py:482
  (69 shorter events, 30.3 us)
Async XLA Ops:
  0.6 41.4 %collective-permute-start.6 = (f32[2,64,4096]{2,1,0:T(8,128)}, f32[2,64,4096]{2,1,0:T(8,128)}, u32[]{:S(2)}, u32[]{:S(2)}) collective-permute-start(f32[2,64,4096]{2,1,0:T(8,128)} %boxes.1), channel_id=1, source_target_pairs={{0,4},{4,0},{8,12},{12,8},{16,20},{20,16},{24,28},{28,24},{32,36},... | collective-permute-start | bytes 6291464 | tf_op jit(solution)/shard_map/ppermute | solution.py:515
  0.7 55.6 %collective-permute-start.5 = (f32[2,64,4096]{2,1,0:T(8,128)}, f32[2,64,4096]{2,1,0:T(8,128)}, u32[]{:S(2)}, u32[]{:S(2)}) collective-permute-start(f32[2,64,4096]{2,1,0:T(8,128)} %boxes.1), channel_id=1, source_target_pairs={{4,8},{8,4},{12,16},{16,12},{20,24},{24,20},{28,32},{32,28},{36,40... | collective-permute-start | bytes 6291464 | tf_op jit(solution)/shard_map/ppermute | solution.py:516
  9.3 23.3 %collective-permute-start.1 = (s32[12]{0:T(128)S(1)}, s32[12]{0:T(128)S(1)}, u32[]{:S(2)}, u32[]{:S(2)}) collective-permute-start(s32[12]{0:T(128)S(1)} %reshape.11), channel_id=1, source_target_pairs={{4,8},{8,4},{12,16},{16,12},{20,24},{24,20},{28,32},{32,28},{36,40... | collective-permute-start | bytes 152 | tf_op jit(solution)/shard_map/ppermute | solution.py:514
  59.7 21.9 %collective-permute-start.13 = (f32[8,64,128]{2,1,0:T(8,128)S(1)}, f32[8,64,128]{2,1,0:T(8,128)S(1)}, u32[]{:S(2)}, u32[]{:S(2)}) collective-permute-start(f32[8,64,128]{2,1,0:T(8,128)S(1)} %get-tuple-element.43), channel_id=1, source_target_pairs={{0,3},{1,2},{2,1},{3,0},{4,7},{5,6},{6,5},{7,4},{8,11},{9,10},{10,... | collective-permute-start | bytes 786440 | tf_op jit(solution)/shard_map/ppermute | solution.py:482
  59.8 23.9 %collective-permute-start.11 = (f32[8,64,128]{2,1,0:T(8,128)S(1)}, f32[8,64,128]{2,1,0:T(8,128)S(1)}, u32[]{:S(2)}, u32[]{:S(2)}) collective-permute-start(f32[8,64,128]{2,1,0:T(8,128)S(1)} %get-tuple-element.41), channel_id=1, source_target_pairs={{0,1},{1,0},{2,3},{3,2},{4,5},{5,4},{6,7},{7,6},{8,9},{9,8},{10,11... | collective-permute-start | bytes 786440 | tf_op jit(solution)/shard_map/ppermute | solution.py:482
  73.8 14.7 %collective-permute-start.9 = (f32[8,64,128]{2,1,0:T(8,128)S(1)}, f32[8,64,128]{2,1,0:T(8,128)S(1)}, u32[]{:S(2)}, u32[]{:S(2)}) collective-permute-start(f32[8,64,128]{2,1,0:T(8,128)S(1)} %get-tuple-element.39), channel_id=1, source_target_pairs={{0,3},{1,2},{2,1},{3,0},{4,7},{5,6},{6,5},{7,4},{8,11},{9,10},{10,... | collective-permute-start | bytes 786440 | tf_op jit(solution)/shard_map/ppermute | solution.py:482
  81.6 10.1 %collective-permute-start.14 = (f32[4,64,128]{2,1,0:T(8,128)S(1)}, f32[4,64,128]{2,1,0:T(8,128)S(1)}, u32[]{:S(2)}, u32[]{:S(2)}) collective-permute-start(f32[4,64,128]{2,1,0:T(8,128)S(1)} %slice_add_fusion), channel_id=1, source_target_pairs={{0,1},{1,0},{2,3},{3,2},{4,5},{5,4},{6,7},{7,6},{8,9},{9,8},{10,11... | collective-permute-start | bytes 393224 | tf_op jit(solution)/shard_map/ppermute | solution.py:482
  98.1 13.8 %collective-permute-start.26 = (f32[8,16,128]{2,1,0:T(8,128)S(1)}, f32[8,16,128]{2,1,0:T(8,128)S(1)}, u32[]{:S(2)}, u32[]{:S(2)}) collective-permute-start(f32[8,16,128]{2,1,0:T(8,128)S(1)} %get-tuple-element.55), channel_id=1, source_target_pairs={{0,8},{4,12},{8,16},{12,20},{16,24},{20,28},{24,32},{28,36},{32,40... | collective-permute-start | bytes 196616 | tf_op jit(solution)/shard_map/ppermute | solution.py:504
  98.1 17.8 %collective-permute-start.27 = (f32[8,16,128]{2,1,0:T(8,128)S(1)}, f32[8,16,128]{2,1,0:T(8,128)S(1)}, u32[]{:S(2)}, u32[]{:S(2)}) collective-permute-start(f32[8,16,128]{2,1,0:T(8,128)S(1)} %get-tuple-element.56), channel_id=1, source_target_pairs={{0,12},{4,16},{8,20},{12,24},{16,28},{20,32},{24,36},{28,40},{32,4... | collective-permute-start | bytes 196616 | tf_op jit(solution)/shard_map/ppermute | solution.py:504
  98.1 20.6 %collective-permute-start.28 = (f32[8,16,128]{2,1,0:T(8,128)S(1)}, f32[8,16,128]{2,1,0:T(8,128)S(1)}, u32[]{:S(2)}, u32[]{:S(2)}) collective-permute-start(f32[8,16,128]{2,1,0:T(8,128)S(1)} %get-tuple-element.57), channel_id=1, source_target_pairs={{0,16},{4,20},{8,24},{12,28},{16,32},{20,36},{24,40},{28,44},{32,4... | collective-permute-start | bytes 196616 | tf_op jit(solution)/shard_map/ppermute | solution.py:504
  103.4 15.3 %collective-permute-start.21 = (f32[8,16,128]{2,1,0:T(8,128)S(1)}, f32[8,16,128]{2,1,0:T(8,128)S(1)}, u32[]{:S(2)}, u32[]{:S(2)}) collective-permute-start(f32[8,16,128]{2,1,0:T(8,128)S(1)} %get-tuple-element.49), channel_id=1, source_target_pairs={{0,4},{4,8},{8,12},{12,16},{16,20},{20,24},{24,28},{28,32},{32,36}... | collective-permute-start | bytes 196616 | tf_op jit(solution)/shard_map/ppermute | solution.py:504
  103.5 15.2 %collective-permute-start.22 = (f32[8,16,128]{2,1,0:T(8,128)S(1)}, f32[8,16,128]{2,1,0:T(8,128)S(1)}, u32[]{:S(2)}, u32[]{:S(2)}) collective-permute-start(f32[8,16,128]{2,1,0:T(8,128)S(1)} %get-tuple-element.50), channel_id=1, source_target_pairs={{0,8},{4,12},{8,16},{12,20},{16,24},{20,28},{24,32},{28,36},{32,40... | collective-permute-start | bytes 196616 | tf_op jit(solution)/shard_map/ppermute | solution.py:504
  111.8 11.0 %collective-permute-start.23 = (f32[8,16,128]{2,1,0:T(8,128)S(1)}, f32[8,16,128]{2,1,0:T(8,128)S(1)}, u32[]{:S(2)}, u32[]{:S(2)}) collective-permute-start(f32[8,16,128]{2,1,0:T(8,128)S(1)} %get-tuple-element.51), channel_id=1, source_target_pairs={{0,12},{4,16},{8,20},{12,24},{16,28},{20,32},{24,36},{28,40},{32,4... | collective-permute-start | bytes 196616 | tf_op jit(solution)/shard_map/ppermute | solution.py:504
  115.8 9.8 %collective-permute-start.24 = (f32[8,16,128]{2,1,0:T(8,128)S(1)}, f32[8,16,128]{2,1,0:T(8,128)S(1)}, u32[]{:S(2)}, u32[]{:S(2)}) collective-permute-start(f32[8,16,128]{2,1,0:T(8,128)S(1)} %get-tuple-element.52), channel_id=1, source_target_pairs={{0,16},{4,20},{8,24},{12,28},{16,32},{20,36},{24,40},{28,44},{32,4... | collective-permute-start | bytes 196616 | tf_op jit(solution)/shard_map/ppermute | solution.py:504
  129.8 18.7 %collective-permute-start.17 = (f32[2,4,64,128]{3,2,1,0:T(8,128)S(1)}, f32[2,4,64,128]{3,2,1,0:T(8,128)S(1)}, u32[]{:S(2)}, u32[]{:S(2)}) collective-permute-start(f32[2,4,64,128]{3,2,1,0:T(8,128)S(1)} %get-tuple-element.46.refs_0_), channel_id=1, source_target_pairs={{0,3},{1,2},{2,1},{3,0},{4,7},{5,6},{6,5},{7,4},{8,11},{9,10},{10,... | collective-permute-start | bytes 786440 | tf_op jit(solution)/shard_map/ppermute | solution.py:482
  131.7 18.3 %collective-permute-start.16 = (f32[2,4,64,128]{3,2,1,0:T(8,128)S(1)}, f32[2,4,64,128]{3,2,1,0:T(8,128)S(1)}, u32[]{:S(2)}, u32[]{:S(2)}) collective-permute-start(f32[2,4,64,128]{3,2,1,0:T(8,128)S(1)} %get-tuple-element.47.refs_1_), channel_id=1, source_target_pairs={{0,1},{1,0},{2,3},{3,2},{4,5},{5,4},{6,7},{7,6},{8,9},{9,8},{10,11... | collective-permute-start | bytes 786440 | tf_op jit(solution)/shard_map/ppermute | solution.py:482
  131.7 12.3 %collective-permute-start.30 = (f32[8,4608]{1,0:T(8,128)S(1)}, f32[8,4608]{1,0:T(8,128)S(1)}, u32[]{:S(2)}, u32[]{:S(2)}) collective-permute-start(f32[8,4608]{1,0:T(8,128)S(1)} %get-tuple-element.59.refs_1_), channel_id=1, source_target_pairs={{0,1},{1,0},{2,3},{3,2},{4,5},{5,4},{6,7},{7,6},{8,9},{9,8},{10,11... | collective-permute-start | bytes 442376 | tf_op jit(solution)/shard_map/ppermute | solution.py:482
  133.7 13.5 %collective-permute-start.29 = (f32[8,4608]{1,0:T(8,128)S(1)}, f32[8,4608]{1,0:T(8,128)S(1)}, u32[]{:S(2)}, u32[]{:S(2)}) collective-permute-start(f32[8,4608]{1,0:T(8,128)S(1)} %get-tuple-element.58.refs_0_), channel_id=1, source_target_pairs={{0,1},{1,0},{2,3},{3,2},{4,5},{5,4},{6,7},{7,6},{8,9},{9,8},{10,11... | collective-permute-start | bytes 442376 | tf_op jit(solution)/shard_map/ppermute | solution.py:482
  136.3 10.8 %collective-permute-start.32 = (f32[8,4608]{1,0:T(8,128)S(1)}, f32[8,4608]{1,0:T(8,128)S(1)}, u32[]{:S(2)}, u32[]{:S(2)}) collective-permute-start(f32[8,4608]{1,0:T(8,128)S(1)} %get-tuple-element.59.refs_1_), channel_id=1, source_target_pairs={{0,3},{1,2},{2,1},{3,0},{4,7},{5,6},{6,5},{7,4},{8,11},{9,10},{10,... | collective-permute-start | bytes 442376 | tf_op jit(solution)/shard_map/ppermute | solution.py:482
  147.2 16.7 %collective-permute-start.15 = (f32[2,4,64,128]{3,2,1,0:T(8,128)S(1)}, f32[2,4,64,128]{3,2,1,0:T(8,128)S(1)}, u32[]{:S(2)}, u32[]{:S(2)}) collective-permute-start(f32[2,4,64,128]{3,2,1,0:T(8,128)S(1)} %get-tuple-element.46.refs_0_), channel_id=1, source_target_pairs={{0,1},{1,0},{2,3},{3,2},{4,5},{5,4},{6,7},{7,6},{8,9},{9,8},{10,11... | collective-permute-start | bytes 786440 | tf_op jit(solution)/shard_map/ppermute | solution.py:482
  147.2 16.7 %collective-permute-start.18 = (f32[2,4,64,128]{3,2,1,0:T(8,128)S(1)}, f32[2,4,64,128]{3,2,1,0:T(8,128)S(1)}, u32[]{:S(2)}, u32[]{:S(2)}) collective-permute-start(f32[2,4,64,128]{3,2,1,0:T(8,128)S(1)} %get-tuple-element.47.refs_1_), channel_id=1, source_target_pairs={{0,3},{1,2},{2,1},{3,0},{4,7},{5,6},{6,5},{7,4},{8,11},{9,10},{10,... | collective-permute-start | bytes 786440 | tf_op jit(solution)/shard_map/ppermute | solution.py:482
  148.5 15.4 %collective-permute-start.19 = (f32[2,4,64,128]{3,2,1,0:T(8,128)S(1)}, f32[2,4,64,128]{3,2,1,0:T(8,128)S(1)}, u32[]{:S(2)}, u32[]{:S(2)}) collective-permute-start(f32[2,4,64,128]{3,2,1,0:T(8,128)S(1)} %collective-permute-done.17.refs_4_), channel_id=1, source_target_pairs={{0,1},{1,0},{2,3},{3,2},{4,5},{5,4},{6,7},{7,6},{8,9},{9,8},{10,11... | collective-permute-start | bytes 786440 | tf_op jit(solution)/shard_map/ppermute | solution.py:482
  149.9 14.0 %collective-permute-start.20 = (f32[2,4,64,128]{3,2,1,0:T(8,128)S(1)}, f32[2,4,64,128]{3,2,1,0:T(8,128)S(1)}, u32[]{:S(2)}, u32[]{:S(2)}) collective-permute-start(f32[2,4,64,128]{3,2,1,0:T(8,128)S(1)} %collective-permute-done.16.refs_3_), channel_id=1, source_target_pairs={{0,3},{1,2},{2,1},{3,0},{4,7},{5,6},{6,5},{7,4},{8,11},{9,10},{10,... | collective-permute-start | bytes 786440 | tf_op jit(solution)/shard_map/ppermute | solution.py:482
  151.8 11.1 %collective-permute-start.34 = (f32[8,4608]{1,0:T(8,128)S(1)}, f32[8,4608]{1,0:T(8,128)S(1)}, u32[]{:S(2)}, u32[]{:S(2)}) collective-permute-start(f32[8,4608]{1,0:T(8,128)S(1)} %collective-permute-done.30.refs_3_), channel_id=1, source_target_pairs={{0,3},{1,2},{2,1},{3,0},{4,7},{5,6},{6,5},{7,4},{8,11},{9,10},{10,... | collective-permute-start | bytes 442376 | tf_op jit(solution)/shard_map/ppermute | solution.py:482
  (13 other events, 100.5 us)

commit v3 on v0

--- a/solution.py
+++ b/solution.py
@@ -82,8 +82,9 @@
     return pl.ds(pl.multiple_of(c * LANES, LANES), LANES)
 
 
-def load_box(own, other, which, write):
-    for boxes, first in ((own, 0), (other, 2)):
+def load_box(groups, which, write):
+    for n, boxes in enumerate(groups):
+        first = 2 * n
 
         @pl.when((which >= first) & (which < first + 2))
         def _():
@@ -94,15 +95,15 @@
             lax.fori_loop(0, COLS, block, 0, unroll=8)
 
 
-def solve_pair(own, other, first, second, delta, within, buffer, still, shifted, basis, image):
+def solve_pair(groups, first, second, delta, within, buffer, still, shifted, basis, image):
     def to_buffer(c, block):
         buffer[c + FRONT, pl.ds(ROOM, BOX), :] = block
 
     def to_still(c, block):
         still[c] = block
 
-    load_box(own, other, first, to_buffer)
-    load_box(own, other, second, to_still)
+    load_box(groups, first, to_buffer)
+    load_box(groups, second, to_still)
     read = shift_reader(buffer, *delta)
     diagonal, coupling = [], []
     norm_before = None
@@ -159,9 +160,9 @@
     return weights
 
 
-def run_pair(own, other, first, second, delta, to_second, to_first, within, forces, *scratch):
+def run_pair(groups, first, second, delta, to_second, to_first, within, forces, *scratch):
     buffer, still, shifted, basis, image = scratch
-    weights = solve_pair(own, other, first, second, delta, within, *scratch)
+    weights = solve_pair(groups, first, second, delta, within, *scratch)
 
     def finish(c, carry):
         potential = weights[0] * basis[0, c + 1, pl.ds(8, BOX), :]
@@ -193,15 +194,21 @@
 
 
 def pairs_kernel(begun, *refs):
+    lists, refs = refs[: 3 if begun else 1], refs[3 if begun else 1 :]
+    offsets, own, *far_away = refs[: 4 if begun else 3]
+    refs = refs[2 + len(far_away) :]
     if begun:
-        lists, offsets, own, other, within, tally, forces_in, *parts, forces = refs[:12]
+        within, tally, forces_in, *parts, forces = refs[:8]
     else:
-        lists, offsets, own, other, within, forces, tally_out = refs[:7]
-    scratch = refs[-5:]
+        within, forces, tally_out = refs[:3]
+    arrived, arrival_sems, table, *scratch = refs[-8:]
     buffer, basis = scratch[0], scratch[3]
     group, mine = place()
     near, far = neighbours(group)
-    neighbour, which = (far, 2) if begun else (near, 1)
+    boxes = [own] + [arrived.at[n] for n in range(len(far_away))]
+    copies = [pltpu.make_async_copy(f, boxes[n + 1], arrival_sems.at[n]) for n, f in enumerate(far_away)]
+    for copy in copies:
+        copy.start()
 
     def clear(c, carry):
         buffer[c] = jnp.zeros((BOX + 2 * ROOM, LANES), jnp.float32)
@@ -211,7 +218,6 @@
     nothing = jnp.zeros((BOX + 16, LANES), jnp.float32)
     for k in range(ITERS):
         basis[k, 0] = nothing
-        basis[k, COLS + 1] = nothing
 
         def clear_ends(c, carry):
             basis[k, c + 1, pl.ds(0, 8), :] = jnp.zeros((8, LANES), jnp.float32)
@@ -227,36 +233,49 @@
 
     lax.fori_loop(0, COLS, open_forces, 0, unroll=2)
 
-    def slot(n, count):
-        foreign = n // 16
-        row = n % 16
-        base = ((row // 4) ^ mine) * 36 + foreign * which * 12 + (row % 4) * 3
-        first = lists[base]
-        second = lists[base + 1]
-        live = lists[base + 2] > 0
-        second_group = second // 2
-        inner = second_group == group
-        outer = second_group == neighbour
-        if begun:
-            wanted = jnp.where(foreign > 0, inner, outer)
-        else:
-            wanted = jnp.where(foreign > 0, inner, inner | outer)
-        taken = live & wanted
-        turn = taken & (lax.rem(count, 4) == mine)
-
-        @pl.when(turn)
-        def _():
-            delta = [offsets[first * 3 + axis] - offsets[second * 3 + axis] for axis in range(3)]
-            first_at = jnp.where(foreign > 0, 2 + first - 2 * neighbour, first - 2 * group)
-            second_at = jnp.where(inner, second - 2 * group, 2 + second - 2 * neighbour)
-            run_pair(own, other, first_at, second_at, delta, inner, foreign == 0, within, forces, *scratch)
-
-        return count + taken.astype(jnp.int32)
-
+    def scan_list(n, slots, carry):
+        def scan(row, carry):
+            count, found = carry
+            base = ((row >> 2) ^ mine) * 12 + (row & 3) * 3
+            first, second, live = slots[base], slots[base + 1], slots[base + 2]
+            second_group = second >> 1
+            if n > 0:
+                wanted = second_group == group
+            elif begun:
+                wanted = second_group == far
+            else:
+                wanted = (second_group == group) | (second_group == near)
+            taken = (live > 0) & wanted
+            table[3 * found] = n
+            table[3 * found + 1] = first
+            table[3 * found + 2] = second
+            found = found + (taken & ((count & 3) == mine)).astype(jnp.int32)
+            return count + taken.astype(jnp.int32), found
+
+        return lax.fori_loop(0, 16, scan, carry, unroll=4)
+
+    carry = (tally[0] if begun else jnp.int32(0), jnp.int32(0))
+    for n, slots in enumerate(lists):
+        carry = scan_list(n, slots, carry)
+    count, found = carry
+    for copy in copies:
+        copy.wait()
+
+    def pair(m, carry):
+        home, first, second = table[3 * m], table[3 * m + 1], table[3 * m + 2]
+        delta = [offsets[first * 3 + axis] - offsets[second * 3 + axis] for axis in range(3)]
+
+        def box_of(orbital):
+            base = jnp.where((orbital >> 1) == group, group, jnp.where((orbital >> 1) == near, near - 1, far - 2))
+            return orbital - 2 * base
+
+        run_pair(boxes, box_of(first), box_of(second), delta, (second >> 1) == group, home == 0, within, forces, *scratch)
+        return carry
+
+    lax.fori_loop(0, found, pair, 0)
     if not begun:
-        tally_out[0] = lax.fori_loop(0, 32, slot, jnp.int32(0))
+        tally_out[0] = count
         return
-    lax.fori_loop(0, 32, slot, tally[0])
     for k, side in enumerate((1, 3)):
         for n, who in enumerate((mine ^ side, mine)):
             for half, quarter in enumerate((who, who ^ (4 - side))):
@@ -288,16 +307,19 @@
     )(boxes)
 
 
-def run_pairs(lists, offsets, own, other, before=None):
+def run_pairs(lists, offsets, own, others, before=None):
     begun = before is not None
-    operands = [lists, offsets, own, other, within_block()]
-    in_specs = [SMEM, SMEM, VMEM, VMEM, VMEM]
+    operands = [*lists, offsets, own, *others, within_block()]
+    in_specs = [SMEM] * (len(lists) + 1) + [VMEM] + [HBM] * len(others) + [VMEM]
     whole = (2, COLS, BOX, LANES)
     scratch = [
+        pltpu.VMEM((len(others), 2, BOX, BOX * BOX), jnp.float32),
+        pltpu.SemaphoreType.DMA((len(others),)),
+        pltpu.SMEM((3 * 64,), jnp.int32),
         pltpu.VMEM((COLS + 2 * FRONT, BOX + 2 * ROOM, LANES), jnp.float32),
         pltpu.VMEM((COLS, BOX, LANES), jnp.float32),
         pltpu.VMEM((COLS, BOX, LANES), jnp.float32),
-        pltpu.VMEM((ITERS, COLS + 2, BOX + 16, LANES), jnp.float32),
+        pltpu.VMEM((ITERS, COLS + 1, BOX + 16, LANES), jnp.float32),
         pltpu.VMEM((COLS, BOX, LANES), jnp.float32),
     ]
     if begun:
@@ -450,8 +472,8 @@
 
 
 def gather_pair(first, second):
-    first_one, first_three = across(first, 1), across(first, 3)
-    second_one, second_three = across(second, 1), across(second, 3)
+    first_three, second_one = across(first, 3), across(second, 1)
+    first_one, second_three = across(first, 1), across(second, 3)
     first_two = across(first_three, 1)
     second_two = across(second_one, 3)
     return [first, second, first_one, second_one, first_three, second_three, first_two, second_two]
@@ -462,16 +484,14 @@
     to_near = [(g, g ^ 1) for g in range(groups)]
     to_far = [(g, neighbours(g)[1]) for g in range(groups) if 0 <= neighbours(g)[1] < groups]
     slots = pair_list.reshape(-1)
-    near_slots = lax.ppermute(slots, "orb", to_near)
-    far_slots = lax.ppermute(slots, "orb", to_far)
+    known = jnp.concatenate([slots] + [across(slots, side) for side in (1, 2, 3)])
     near = lax.ppermute(orbitals, "orb", to_near)
     far = lax.ppermute(orbitals, "orb", to_far)
-    known = jnp.concatenate([slots, near_slots, far_slots])
-    lists = jnp.concatenate([known] + [across(known, side) for side in (1, 2, 3)])
+    lists = [known, lax.ppermute(known, "orb", to_near), lax.ppermute(known, "orb", to_far)]
     offsets = box_offsets.reshape(-1)
     own = stage(orbitals)
-    before = run_pairs(lists, offsets, own, near)
-    sent_zero, kept_zero, sent_one, kept_one = run_pairs(lists, offsets, own, far, before)
+    before = run_pairs(lists[:1], offsets, own, [near])
+    sent_zero, kept_zero, sent_one, kept_one = run_pairs(lists, offsets, own, [near, far], before)
     got_zero, got_one = across(sent_zero, 1), across(sent_one, 3)
     last_zero = across(kept_zero[QUARTER:] + got_zero[QUARTER:], 3)
     last_one = across(kept_one[QUARTER:] + got_one[QUARTER:], 1)

time: 147 us -> 131 us (0.89)
  waiting for transfers between devices: 70.9 us -> 43.4 us
  starting transfers between devices: 41.7 us -> 55.7 us
  Pallas kernels: 29.9 us -> 27.2 us
    ppermute x2, waiting for transfers between devices: 18.5 us -> 0.23 us  [the longest x1 0.23 us: shards(): lax.ppermute(known, 'orb', to_far)]
    ppermute x19, starting transfers between devices: 24.2 us -> 40 us  [across(): lax.ppermute(block, 'rep', [(i, i ^ side) for i in range(lax.axis_size('r...]
    ppermute x19, waiting for transfers between devices: 35.6 us -> 25.7 us  [across(): lax.ppermute(block, 'rep', [(i, i ^ side) for i in range(lax.axis_size('r...]
    pallas_call x2, Pallas kernels: 23.9 us -> 21.2 us  [run_pairs(): pl.pallas_call(functools.partial(pairs_kernel, begun), out_shape=out_shap...]
    ppermute x4, starting transfers between devices: 7.56 us -> 5.74 us  [shards(): pieces.append(lax.ppermute(settled[2 + later], 'orb', route))]
  transfers between devices with their start and end apart: 27 -> 27, of which waited for: 12 -> 12; matrix products, arithmetic and copies ran while one was open for 1% -> 1% of each run, Pallas kernels for 12% -> 13%
where the time goes in v3:
time: 131 us
  starting transfers between devices  55.7 us (43%)
  waiting for transfers between devices  43.4 us (33%)
  Pallas kernels  27.2 us (21%)
  local copies, waits for them, and re-layouts  3.35 us (3%)
    ppermute x19, starting transfers between devices, across(): lax.ppermute(block, 'rep', [(i, i ^ side) for i in range(lax.axis_size('r...  40 us
    ppermute x19, waiting for transfers between devices, across(): lax.ppermute(block, 'rep', [(i, i ^ side) for i in range(lax.axis_size('r...  25.7 us
    pallas_call x2, Pallas kernels, run_pairs(): pl.pallas_call(functools.partial(pairs_kernel, begun), out_shape=out_shap...  21.2 us
    ppermute x4, waiting for transfers between devices, shards(): pieces.append(lax.ppermute(settled[2 + later], 'orb', route))  17.5 us
    ppermute x1, starting transfers between devices, shards(): far = lax.ppermute(orbitals, 'orb', to_far)  7.83 us
    ppermute x4, starting transfers between devices, shards(): pieces.append(lax.ppermute(settled[2 + later], 'orb', route))  5.74 us
    pallas_call x1, Pallas kernels, deposit(): pl.pallas_call(deposit_kernel, out_shape=[half] * 2, in_specs=[SMEM] + [V...  2.68 us
  transfers between devices with their start and end apart: 27, of which 12 were waited for; matrix products, arithmetic and copies ran while one was open for 1% of the time, Pallas kernels for 13%

profile of v3, /device:TPU:4, one launch (start us, length us, event | category | flops | bytes accessed | tf_op | source)
XLA Modules:
  0.0 130.5 jit_solution(17904575631912659969)
XLA Ops:
  0.7 7.8 %collective-permute-start.6 = (f32[2,64,4096]{2,1,0:T(8,128)}, f32[2,64,4096]{2,1,0:T(8,128)}, u32[]{:S(2)}, u32[]{:S(2)}) collective-permute-start(f32[2,64,4096]{2,1,0:T(8,128)} %boxes.1), channel_id=1, source_target_pairs={{4,8},{8,4},{12,16},{16,12},{20,24},{24,20},{28,32},{32,28},{36,40... | collective-permute-start | bytes 6291464 | tf_op jit(solution)/shard_map/ppermute | solution.py:489
  9.3 3.0 %collective-permute-start.2 = (s32[12]{0:T(128)S(1)}, s32[12]{0:T(128)S(1)}, u32[]{:S(2)}, u32[]{:S(2)}) collective-permute-start(s32[12]{0:T(128)S(1)} %reshape.11), channel_id=1, source_target_pairs={{0,3},{1,2},{2,1},{3,0},{4,7},{5,6},{6,5},{7,4},{8,11},{9,10},{10,... | collective-permute-start | bytes 152 | tf_op jit(solution)/shard_map/ppermute | solution.py:471
  14.4 1.6 %copy-done = f32[2,64,4096]{2,1,0:T(8,128)S(1)} copy-done((f32[2,64,4096]{2,1,0:T(8,128)S(1)}, f32[2,64,4096]{2,1,0:T(8,128)}, u32[]{:S(2)}) %copy-start) | copy-done | bytes 2097176
  17.5 1.9 %collective-permute-start.4 = (s32[48]{0:T(128)S(1)}, s32[48]{0:T(128)S(1)}, u32[]{:S(2)}, u32[]{:S(2)}) collective-permute-start(s32[48]{0:T(128)S(1)} %pad_add_fusion.refs_0_), channel_id=1, source_target_pairs={{4,8},{8,4},{12,16},{16,12},{20,24},{24,20},{28,32},{32,28},{36,40... | collective-permute-start | bytes 584 | tf_op jit(solution)/shard_map/ppermute | solution.py:490
  19.5 12.8 %pairs_near.1 = (f32[2,32,64,128]{3,2,1,0:T(8,128)S(1)}, s32[1]{0:T(128)}) custom-call(s32[48]{0:T(128)S(1)} %pad_add_fusion.refs_0_, s32[384]{0:T(512)S(1)} %reshape.10.refs_1_.refs_3_.offsets, f32[2,64,4096]{2,1,0:T(8,128)S(1)} %stage.1.refs_2_.refs_4_, f32[2,64,4096]{2,1,0:T(8,128)S(1)} %collective-permute-done.5.refs_3_.refs_5_, ...), custom_call_target="tpu_custom_call" | custom-call | flops 100000000 | bytes 8388608 | tf_op jit(solution)/shard_map/pairs_near/pallas_call | solution.py:334
  32.6 8.4 %pairs_far.1 = (f32[16,64,128]{2,1,0:T(8,128)S(1)}, f32[16,64,128]{2,1,0:T(8,128)S(1)}, f32[16,64,128]{2,1,0:T(8,128)S(1)}, f32[16,64,128]{2,1,0:T(8,128)S(1)}) custom-call(s32[48]{0:T(128)S(1)} %pad_add_fusion.refs_0_, s32[48]{0:T(128)S(1)} %collective-permute-done.3.refs_1_, s32[48]{0:T(128)S(1)} %collective-permute-done.4.refs_2_, ...), custom_call_target="tpu_custom_call" | custom-call | flops 100000000 | bytes 8388608 | tf_op jit(solution)/shard_map/pairs_far/pallas_call | solution.py:334
  42.5 7.5 %collective-permute-start.9 = (f32[16,64,128]{2,1,0:T(8,128)S(1)}, f32[16,64,128]{2,1,0:T(8,128)S(1)}, u32[]{:S(2)}, u32[]{:S(2)}) collective-permute-start(f32[16,64,128]{2,1,0:T(8,128)S(1)} %get-tuple-element.22), channel_id=1, source_target_pairs={{0,3},{1,2},{2,1},{3,0},{4,7},{5,6},{6,5},{7,4},{8,11},{9,10},{10,... | collective-permute-start | bytes 1572872 | tf_op jit(solution)/shard_map/ppermute | solution.py:471
  50.5 13.1 %collective-permute-start.8 = (f32[8,64,128]{2,1,0:T(8,128)S(1)}, f32[8,64,128]{2,1,0:T(8,128)S(1)}, u32[]{:S(2)}, u32[]{:S(2)}) collective-permute-start(f32[8,64,128]{2,1,0:T(8,128)S(1)} %slice_add_fusion.1), channel_id=1, source_target_pairs={{0,3},{1,2},{2,1},{3,0},{4,7},{5,6},{6,5},{7,4},{8,11},{9,10},{10,... | collective-permute-start | bytes 786440 | tf_op jit(solution)/shard_map/ppermute | solution.py:471
  63.8 6.9 %collective-permute-done.8.refs_2_ = f32[8,64,128]{2,1,0:T(8,128)S(1)} collective-permute-done((f32[8,64,128]{2,1,0:T(8,128)S(1)}, f32[8,64,128]{2,1,0:T(8,128)S(1)}, u32[]{:S(2)}, u32[]{:S(2)}) %collective-permute-start.8) | collective-permute-done | bytes 262176 | tf_op jit(solution)/shard_map/ppermute | solution.py:471
  70.7 1.6 %collective-permute-done.10.refs_5_ = f32[8,64,128]{2,1,0:T(8,128)S(1)} collective-permute-done((f32[8,64,128]{2,1,0:T(8,128)S(1)}, f32[8,64,128]{2,1,0:T(8,128)S(1)}, u32[]{:S(2)}, u32[]{:S(2)}) %collective-permute-start.10) | collective-permute-done | bytes 262176 | tf_op jit(solution)/shard_map/ppermute | solution.py:471
  73.0 1.9 %collective-permute-start.13 = (f32[8,64,128]{2,1,0:T(8,128)S(1)}, f32[8,64,128]{2,1,0:T(8,128)S(1)}, u32[]{:S(2)}, u32[]{:S(2)}) collective-permute-start(f32[8,64,128]{2,1,0:T(8,128)S(1)} %get-tuple-element.23.refs_0_), channel_id=1, source_target_pairs={{0,3},{1,2},{2,1},{3,0},{4,7},{5,6},{6,5},{7,4},{8,11},{9,10},{10,... | collective-permute-start | bytes 786440 | tf_op jit(solution)/shard_map/ppermute | solution.py:471
  76.4 2.5 %collective-permute-start.19 = (f32[2,8,16,128]{3,2,1,0:T(8,128)S(1)}, f32[2,8,16,128]{3,2,1,0:T(8,128)S(1)}, u32[]{:S(2)}, u32[]{:S(2)}) collective-permute-start(f32[2,8,16,128]{3,2,1,0:T(8,128)S(1)} %get-tuple-element.28), channel_id=1, source_target_pairs={{0,12},{4,16},{8,20},{12,24},{16,28},{20,32},{24,36},{28,40},{32,4... | collective-permute-start | bytes 393224 | tf_op jit(solution)/shard_map/ppermute | solution.py:502
  78.8 1.8 %collective-permute-start.20 = (f32[2,8,16,128]{3,2,1,0:T(8,128)S(1)}, f32[2,8,16,128]{3,2,1,0:T(8,128)S(1)}, u32[]{:S(2)}, u32[]{:S(2)}) collective-permute-start(f32[2,8,16,128]{3,2,1,0:T(8,128)S(1)} %get-tuple-element.29), channel_id=1, source_target_pairs={{0,16},{4,20},{8,24},{12,28},{16,32},{20,36},{24,40},{28,44},{32,4... | collective-permute-start | bytes 393224 | tf_op jit(solution)/shard_map/ppermute | solution.py:502
  80.6 2.9 %collective-permute-done.17.refs_1_ = f32[2,8,16,128]{3,2,1,0:T(8,128)S(1)} collective-permute-done((f32[2,8,16,128]{3,2,1,0:T(8,128)S(1)}, f32[2,8,16,128]{3,2,1,0:T(8,128)S(1)}, u32[]{:S(2)}, u32[]{:S(2)}) %collective-permute-start.17) | collective-permute-done | bytes 131104 | tf_op jit(solution)/shard_map/ppermute | solution.py:502
  83.6 3.3 %collective-permute-done.18.refs_2_ = f32[2,8,16,128]{3,2,1,0:T(8,128)S(1)} collective-permute-done((f32[2,8,16,128]{3,2,1,0:T(8,128)S(1)}, f32[2,8,16,128]{3,2,1,0:T(8,128)S(1)}, u32[]{:S(2)}, u32[]{:S(2)}) %collective-permute-start.18) | collective-permute-done | bytes 131104 | tf_op jit(solution)/shard_map/ppermute | solution.py:502
  86.9 8.6 %collective-permute-done.19.refs_3_ = f32[2,8,16,128]{3,2,1,0:T(8,128)S(1)} collective-permute-done((f32[2,8,16,128]{3,2,1,0:T(8,128)S(1)}, f32[2,8,16,128]{3,2,1,0:T(8,128)S(1)}, u32[]{:S(2)}, u32[]{:S(2)}) %collective-permute-start.19) | collective-permute-done | bytes 131104 | tf_op jit(solution)/shard_map/ppermute | solution.py:502
  95.5 2.7 %collective-permute-done.20.refs_4_ = f32[2,8,16,128]{3,2,1,0:T(8,128)S(1)} collective-permute-done((f32[2,8,16,128]{3,2,1,0:T(8,128)S(1)}, f32[2,8,16,128]{3,2,1,0:T(8,128)S(1)}, u32[]{:S(2)}, u32[]{:S(2)}) %collective-permute-start.20) | collective-permute-done | bytes 131104 | tf_op jit(solution)/shard_map/ppermute | solution.py:502
  98.2 2.7 %deposit.1 = (f32[8,4608]{1,0:T(8,128)S(1)}, f32[8,4608]{1,0:T(8,128)S(1)}) custom-call(s32[384]{0:T(512)S(1)} %reshape.10.refs_1_.refs_3_.offsets, f32[2,8,16,128]{3,2,1,0:T(8,128)S(1)} %get-tuple-element.25.refs_0_, f32[2,8,16,128]{3,2,1,0:T(8,128)S(1)} %collective-permute-done.17.refs_1_, f32[2,8,16,128]{3,2,1,0:T(8,128)S(1)} %collective-permute-done.18.refs_2_, ...), custom_call_target="tpu_custom_call" | custom-call | flops 8000000 | bytes 2097152 | tf_op jit(solution)/shard_map/deposit/pallas_call | solution.py:409
  102.0 2.2 %collective-permute-start.24 = (f32[8,4608]{1,0:T(8,128)S(1)}, f32[8,4608]{1,0:T(8,128)S(1)}, u32[]{:S(2)}, u32[]{:S(2)}) collective-permute-start(f32[8,4608]{1,0:T(8,128)S(1)} %get-tuple-element.31.refs_1_), channel_id=1, source_target_pairs={{0,3},{1,2},{2,1},{3,0},{4,7},{5,6},{6,5},{7,4},{8,11},{9,10},{10,... | collective-permute-start | bytes 442376 | tf_op jit(solution)/shard_map/ppermute | solution.py:471
  105.6 3.3 %collective-permute-done.23.refs_4_ = f32[8,4608]{1,0:T(8,128)S(1)} collective-permute-done((f32[8,4608]{1,0:T(8,128)S(1)}, f32[8,4608]{1,0:T(8,128)S(1)}, u32[]{:S(2)}, u32[]{:S(2)}) %collective-permute-start.23) | collective-permute-done | bytes 147488 | tf_op jit(solution)/shard_map/ppermute | solution.py:471
  108.9 2.0 %collective-permute-start.11 = (f32[8,64,128]{2,1,0:T(8,128)S(1)}, f32[8,64,128]{2,1,0:T(8,128)S(1)}, u32[]{:S(2)}, u32[]{:S(2)}) collective-permute-start(f32[8,64,128]{2,1,0:T(8,128)S(1)} %get-tuple-element.23.refs_0_), channel_id=1, source_target_pairs={{0,1},{1,0},{2,3},{3,2},{4,5},{5,4},{6,7},{7,6},{8,9},{9,8},{10,11... | collective-permute-start | bytes 786440 | tf_op jit(solution)/shard_map/ppermute | solution.py:471
  112.0 2.3 %collective-permute-start.16 = (f32[8,64,128]{2,1,0:T(8,128)S(1)}, f32[8,64,128]{2,1,0:T(8,128)S(1)}, u32[]{:S(2)}, u32[]{:S(2)}) collective-permute-start(f32[8,64,128]{2,1,0:T(8,128)S(1)} %collective-permute-done.12.refs_3_), channel_id=1, source_target_pairs={{0,3},{1,2},{2,1},{3,0},{4,7},{5,6},{6,5},{7,4},{8,11},{9,10},{10,... | collective-permute-start | bytes 786440 | tf_op jit(solution)/shard_map/ppermute | solution.py:471
  115.6 1.6 %collective-permute-start.26 = (f32[8,4608]{1,0:T(8,128)S(1)}, f32[8,4608]{1,0:T(8,128)S(1)}, u32[]{:S(2)}, u32[]{:S(2)}) collective-permute-start(f32[8,4608]{1,0:T(8,128)S(1)} %collective-permute-done.22.refs_3_), channel_id=1, source_target_pairs={{0,3},{1,2},{2,1},{3,0},{4,7},{5,6},{6,5},{7,4},{8,11},{9,10},{10,... | collective-permute-start | bytes 442376 | tf_op jit(solution)/shard_map/ppermute | solution.py:471
  117.2 10.8 %collective-permute-done.26.refs_7_ = f32[8,4608]{1,0:T(8,128)S(1)} collective-permute-done((f32[8,4608]{1,0:T(8,128)S(1)}, f32[8,4608]{1,0:T(8,128)S(1)}, u32[]{:S(2)}, u32[]{:S(2)}) %collective-permute-start.26) | collective-permute-done | bytes 147488 | tf_op jit(solution)/shard_map/ppermute | solution.py:471
  (47 shorter events, 16.5 us)
Async XLA Ops:
  0.6 18.9 %collective-permute-start.5 = (f32[2,64,4096]{2,1,0:T(8,128)}, f32[2,64,4096]{2,1,0:T(8,128)S(1)}, u32[]{:S(2)}, u32[]{:S(2)}) collective-permute-start(f32[2,64,4096]{2,1,0:T(8,128)} %boxes.1), channel_id=1, source_target_pairs={{0,4},{4,0},{8,12},{12,8},{16,20},{20,16},{24,28},{28,24},{32,36},... | collective-permute-start | bytes 6291464 | tf_op jit(solution)/shard_map/ppermute | solution.py:488
  0.7 31.9 %collective-permute-start.6 = (f32[2,64,4096]{2,1,0:T(8,128)}, f32[2,64,4096]{2,1,0:T(8,128)}, u32[]{:S(2)}, u32[]{:S(2)}) collective-permute-start(f32[2,64,4096]{2,1,0:T(8,128)} %boxes.1), channel_id=1, source_target_pairs={{4,8},{8,4},{12,16},{16,12},{20,24},{24,20},{28,32},{32,28},{36,40... | collective-permute-start | bytes 6291464 | tf_op jit(solution)/shard_map/ppermute | solution.py:489
  9.3 6.8 %collective-permute-start.2 = (s32[12]{0:T(128)S(1)}, s32[12]{0:T(128)S(1)}, u32[]{:S(2)}, u32[]{:S(2)}) collective-permute-start(s32[12]{0:T(128)S(1)} %reshape.11), channel_id=1, source_target_pairs={{0,3},{1,2},{2,1},{3,0},{4,7},{5,6},{6,5},{7,4},{8,11},{9,10},{10,... | collective-permute-start | bytes 152 | tf_op jit(solution)/shard_map/ppermute | solution.py:471
  17.5 15.1 %collective-permute-start.4 = (s32[48]{0:T(128)S(1)}, s32[48]{0:T(128)S(1)}, u32[]{:S(2)}, u32[]{:S(2)}) collective-permute-start(s32[48]{0:T(128)S(1)} %pad_add_fusion.refs_0_), channel_id=1, source_target_pairs={{4,8},{8,4},{12,16},{16,12},{20,24},{24,20},{28,32},{32,28},{36,40... | collective-permute-start | bytes 584 | tf_op jit(solution)/shard_map/ppermute | solution.py:490
  19.4 13.2 %collective-permute-start.3 = (s32[48]{0:T(128)S(1)}, s32[48]{0:T(128)S(1)}, u32[]{:S(2)}, u32[]{:S(2)}) collective-permute-start(s32[48]{0:T(128)S(1)} %pad_add_fusion.refs_0_), channel_id=1, source_target_pairs={{0,4},{4,0},{8,12},{12,8},{16,20},{20,16},{24,28},{28,24},{32,36},... | collective-permute-start | bytes 584 | tf_op jit(solution)/shard_map/ppermute | solution.py:490
  41.0 9.4 %collective-permute-start.7 = (f32[16,64,128]{2,1,0:T(8,128)S(1)}, f32[16,64,128]{2,1,0:T(8,128)S(1)}, u32[]{:S(2)}, u32[]{:S(2)}) collective-permute-start(f32[16,64,128]{2,1,0:T(8,128)S(1)} %get-tuple-element.20), channel_id=1, source_target_pairs={{0,1},{1,0},{2,3},{3,2},{4,5},{5,4},{6,7},{7,6},{8,9},{9,8},{10,11... | collective-permute-start | bytes 1572872 | tf_op jit(solution)/shard_map/ppermute | solution.py:471
  42.5 21.1 %collective-permute-start.9 = (f32[16,64,128]{2,1,0:T(8,128)S(1)}, f32[16,64,128]{2,1,0:T(8,128)S(1)}, u32[]{:S(2)}, u32[]{:S(2)}) collective-permute-start(f32[16,64,128]{2,1,0:T(8,128)S(1)} %get-tuple-element.22), channel_id=1, source_target_pairs={{0,3},{1,2},{2,1},{3,0},{4,7},{5,6},{6,5},{7,4},{8,11},{9,10},{10,... | collective-permute-start | bytes 1572872 | tf_op jit(solution)/shard_map/ppermute | solution.py:471
  50.5 20.2 %collective-permute-start.8 = (f32[8,64,128]{2,1,0:T(8,128)S(1)}, f32[8,64,128]{2,1,0:T(8,128)S(1)}, u32[]{:S(2)}, u32[]{:S(2)}) collective-permute-start(f32[8,64,128]{2,1,0:T(8,128)S(1)} %slice_add_fusion.1), channel_id=1, source_target_pairs={{0,3},{1,2},{2,1},{3,0},{4,7},{5,6},{6,5},{7,4},{8,11},{9,10},{10,... | collective-permute-start | bytes 786440 | tf_op jit(solution)/shard_map/ppermute | solution.py:471
  63.6 8.7 %collective-permute-start.10 = (f32[8,64,128]{2,1,0:T(8,128)S(1)}, f32[8,64,128]{2,1,0:T(8,128)S(1)}, u32[]{:S(2)}, u32[]{:S(2)}) collective-permute-start(f32[8,64,128]{2,1,0:T(8,128)S(1)} %slice_add_fusion), channel_id=1, source_target_pairs={{0,1},{1,0},{2,3},{3,2},{4,5},{5,4},{6,7},{7,6},{8,9},{9,8},{10,11... | collective-permute-start | bytes 786440 | tf_op jit(solution)/shard_map/ppermute | solution.py:471
  73.0 31.2 %collective-permute-start.13 = (f32[8,64,128]{2,1,0:T(8,128)S(1)}, f32[8,64,128]{2,1,0:T(8,128)S(1)}, u32[]{:S(2)}, u32[]{:S(2)}) collective-permute-start(f32[8,64,128]{2,1,0:T(8,128)S(1)} %get-tuple-element.23.refs_0_), channel_id=1, source_target_pairs={{0,3},{1,2},{2,1},{3,0},{4,7},{5,6},{6,5},{7,4},{8,11},{9,10},{10,... | collective-permute-start | bytes 786440 | tf_op jit(solution)/shard_map/ppermute | solution.py:471
  74.9 8.7 %collective-permute-start.17 = (f32[2,8,16,128]{3,2,1,0:T(8,128)S(1)}, f32[2,8,16,128]{3,2,1,0:T(8,128)S(1)}, u32[]{:S(2)}, u32[]{:S(2)}) collective-permute-start(f32[2,8,16,128]{3,2,1,0:T(8,128)S(1)} %get-tuple-element.26), channel_id=1, source_target_pairs={{0,4},{4,8},{8,12},{12,16},{16,20},{20,24},{24,28},{28,32},{32,36}... | collective-permute-start | bytes 393224 | tf_op jit(solution)/shard_map/ppermute | solution.py:502
  74.9 12.0 %collective-permute-start.18 = (f32[2,8,16,128]{3,2,1,0:T(8,128)S(1)}, f32[2,8,16,128]{3,2,1,0:T(8,128)S(1)}, u32[]{:S(2)}, u32[]{:S(2)}) collective-permute-start(f32[2,8,16,128]{3,2,1,0:T(8,128)S(1)} %get-tuple-element.27), channel_id=1, source_target_pairs={{0,8},{4,12},{8,16},{12,20},{16,24},{20,28},{24,32},{28,36},{32,40... | collective-permute-start | bytes 393224 | tf_op jit(solution)/shard_map/ppermute | solution.py:502
  76.4 19.1 %collective-permute-start.19 = (f32[2,8,16,128]{3,2,1,0:T(8,128)S(1)}, f32[2,8,16,128]{3,2,1,0:T(8,128)S(1)}, u32[]{:S(2)}, u32[]{:S(2)}) collective-permute-start(f32[2,8,16,128]{3,2,1,0:T(8,128)S(1)} %get-tuple-element.28), channel_id=1, source_target_pairs={{0,12},{4,16},{8,20},{12,24},{16,28},{20,32},{24,36},{28,40},{32,4... | collective-permute-start | bytes 393224 | tf_op jit(solution)/shard_map/ppermute | solution.py:502
  78.8 19.4 %collective-permute-start.20 = (f32[2,8,16,128]{3,2,1,0:T(8,128)S(1)}, f32[2,8,16,128]{3,2,1,0:T(8,128)S(1)}, u32[]{:S(2)}, u32[]{:S(2)}) collective-permute-start(f32[2,8,16,128]{3,2,1,0:T(8,128)S(1)} %get-tuple-element.29), channel_id=1, source_target_pairs={{0,16},{4,20},{8,24},{12,28},{16,32},{20,36},{24,40},{28,44},{32,4... | collective-permute-start | bytes 393224 | tf_op jit(solution)/shard_map/ppermute | solution.py:502
  83.6 25.3 %collective-permute-start.12 = (f32[8,64,128]{2,1,0:T(8,128)S(1)}, f32[8,64,128]{2,1,0:T(8,128)S(1)}, u32[]{:S(2)}, u32[]{:S(2)}) collective-permute-start(f32[8,64,128]{2,1,0:T(8,128)S(1)} %get-tuple-element.24.refs_1_), channel_id=1, source_target_pairs={{0,1},{1,0},{2,3},{3,2},{4,5},{5,4},{6,7},{7,6},{8,9},{9,8},{10,11... | collective-permute-start | bytes 786440 | tf_op jit(solution)/shard_map/ppermute | solution.py:471
  100.9 8.0 %collective-permute-start.23 = (f32[8,4608]{1,0:T(8,128)S(1)}, f32[8,4608]{1,0:T(8,128)S(1)}, u32[]{:S(2)}, u32[]{:S(2)}) collective-permute-start(f32[8,4608]{1,0:T(8,128)S(1)} %get-tuple-element.30.refs_0_), channel_id=1, source_target_pairs={{0,3},{1,2},{2,1},{3,0},{4,7},{5,6},{6,5},{7,4},{8,11},{9,10},{10,... | collective-permute-start | bytes 442376 | tf_op jit(solution)/shard_map/ppermute | solution.py:471
  102.0 8.9 %collective-permute-start.21 = (f32[8,4608]{1,0:T(8,128)S(1)}, f32[8,4608]{1,0:T(8,128)S(1)}, u32[]{:S(2)}, u32[]{:S(2)}) collective-permute-start(f32[8,4608]{1,0:T(8,128)S(1)} %get-tuple-element.30.refs_0_), channel_id=1, source_target_pairs={{0,1},{1,0},{2,3},{3,2},{4,5},{5,4},{6,7},{7,6},{8,9},{9,8},{10,11... | collective-permute-start | bytes 442376 | tf_op jit(solution)/shard_map/ppermute | solution.py:471
  102.0 10.0 %collective-permute-start.24 = (f32[8,4608]{1,0:T(8,128)S(1)}, f32[8,4608]{1,0:T(8,128)S(1)}, u32[]{:S(2)}, u32[]{:S(2)}) collective-permute-start(f32[8,4608]{1,0:T(8,128)S(1)} %get-tuple-element.31.refs_1_), channel_id=1, source_target_pairs={{0,3},{1,2},{2,1},{3,0},{4,7},{5,6},{6,5},{7,4},{8,11},{9,10},{10,... | collective-permute-start | bytes 442376 | tf_op jit(solution)/shard_map/ppermute | solution.py:471
  104.2 7.8 %collective-permute-start.22 = (f32[8,4608]{1,0:T(8,128)S(1)}, f32[8,4608]{1,0:T(8,128)S(1)}, u32[]{:S(2)}, u32[]{:S(2)}) collective-permute-start(f32[8,4608]{1,0:T(8,128)S(1)} %get-tuple-element.31.refs_1_), channel_id=1, source_target_pairs={{0,1},{1,0},{2,3},{3,2},{4,5},{5,4},{6,7},{7,6},{8,9},{9,8},{10,11... | collective-permute-start | bytes 442376 | tf_op jit(solution)/shard_map/ppermute | solution.py:471
  108.9 20.1 %collective-permute-start.11 = (f32[8,64,128]{2,1,0:T(8,128)S(1)}, f32[8,64,128]{2,1,0:T(8,128)S(1)}, u32[]{:S(2)}, u32[]{:S(2)}) collective-permute-start(f32[8,64,128]{2,1,0:T(8,128)S(1)} %get-tuple-element.23.refs_0_), channel_id=1, source_target_pairs={{0,1},{1,0},{2,3},{3,2},{4,5},{5,4},{6,7},{7,6},{8,9},{9,8},{10,11... | collective-permute-start | bytes 786440 | tf_op jit(solution)/shard_map/ppermute | solution.py:471
  110.9 18.1 %collective-permute-start.14 = (f32[8,64,128]{2,1,0:T(8,128)S(1)}, f32[8,64,128]{2,1,0:T(8,128)S(1)}, u32[]{:S(2)}, u32[]{:S(2)}) collective-permute-start(f32[8,64,128]{2,1,0:T(8,128)S(1)} %get-tuple-element.24.refs_1_), channel_id=1, source_target_pairs={{0,3},{1,2},{2,1},{3,0},{4,7},{5,6},{6,5},{7,4},{8,11},{9,10},{10,... | collective-permute-start | bytes 786440 | tf_op jit(solution)/shard_map/ppermute | solution.py:471
  112.0 17.1 %collective-permute-start.15 = (f32[8,64,128]{2,1,0:T(8,128)S(1)}, f32[8,64,128]{2,1,0:T(8,128)S(1)}, u32[]{:S(2)}, u32[]{:S(2)}) collective-permute-start(f32[8,64,128]{2,1,0:T(8,128)S(1)} %collective-permute-done.13.refs_4_), channel_id=1, source_target_pairs={{0,1},{1,0},{2,3},{3,2},{4,5},{5,4},{6,7},{7,6},{8,9},{9,8},{10,11... | collective-permute-start | bytes 786440 | tf_op jit(solution)/shard_map/ppermute | solution.py:471
  112.0 17.0 %collective-permute-start.16 = (f32[8,64,128]{2,1,0:T(8,128)S(1)}, f32[8,64,128]{2,1,0:T(8,128)S(1)}, u32[]{:S(2)}, u32[]{:S(2)}) collective-permute-start(f32[8,64,128]{2,1,0:T(8,128)S(1)} %collective-permute-done.12.refs_3_), channel_id=1, source_target_pairs={{0,3},{1,2},{2,1},{3,0},{4,7},{5,6},{6,5},{7,4},{8,11},{9,10},{10,... | collective-permute-start | bytes 786440 | tf_op jit(solution)/shard_map/ppermute | solution.py:471
  115.6 12.4 %collective-permute-start.26 = (f32[8,4608]{1,0:T(8,128)S(1)}, f32[8,4608]{1,0:T(8,128)S(1)}, u32[]{:S(2)}, u32[]{:S(2)}) collective-permute-start(f32[8,4608]{1,0:T(8,128)S(1)} %collective-permute-done.22.refs_3_), channel_id=1, source_target_pairs={{0,3},{1,2},{2,1},{3,0},{4,7},{5,6},{6,5},{7,4},{8,11},{9,10},{10,... | collective-permute-start | bytes 442376 | tf_op jit(solution)/shard_map/ppermute | solution.py:471
  (5 other events, 21.3 us)
